TPU v7x, 256 devices: a whole 4x4x8 slice. The times are simulated.
256 devices in a mesh: gx: 16 (over z, core), gy: 4 (over y), gz: 4 (over x).
Axes of the slice: x: 4, y: 4, z: 8, core: 2. Of those that a mesh axis runs over, the one named last changes fastest.
Arguments:
- right_side: float32 [128, 64, 1024], P('gx', 'gy', 'gz'), may hold values from -8 to 8
- outer_diag: float32 [128, 64, 1024], P('gx', 'gy', 'gz'), may hold values from 0.25 to 2
- stencil_nodes: int32 [2097152], P(('gx', 'gy', 'gz')), may hold values from 0 to 28414
- stencil_weights: float32 [8, 2097152], P(None, ('gx', 'gy', 'gz')), may hold values from -4.2 to 4.2
- handover_dest: int32 [2097152, 1], P(('gx', 'gy', 'gz')), may hold values from 0 to 63; in each aligned block of 8192 rows (0 to 8191, 8192 to 16383, ...) at most 256 rows name the same one
- handover_cell: int32 [2097152], P(('gx', 'gy', 'gz')), may hold values from 0 to 65535
- pressure_prev: float32 [128, 128, 1024], P('gx', 'gy', 'gz'), may hold values from -6 to 6
- inner_source: float32 [128, 128, 1024], P('gx', 'gy', 'gz'), may hold values from -6 to 6
- inner_diag: float32 [128, 128, 1024], P('gx', 'gy', 'gz'), may hold values from 0.25 to 2
Outputs:
- solution_field: float32 [128, 64, 1024], P('gx', 'gy', 'gz')
- residual: float32 [128, 64, 1024], P('gx', 'gy', 'gz')
- pressure: float32 [128, 128, 1024], P('gx', 'gy', 'gz')
Inputs may be any that keep to these rules, and one draw needn't show every extreme that they name: `handover_dest`: among the 8192 points of one device, at most 256 go to one destination, and some destination gets exactly 256.
All inputs are finite; a program needn't handle non-finite values.
Results may differ from a plain program's by a relative error of at most 0.00018.
Values sent between devices are 32-bit elements; how exact they have to be, the bound alone decides.
A program may use at most 64 MiB of HBM per device.

v0:
```python
import jax
import jax.numpy as jnp
from jax import lax
from jax.sharding import PartitionSpec as P

ITERS = 2
SWEEPS = 2


def padded_2(cells, sides, width):
    for axis, dim in sides:
        count = lax.axis_size(axis)
        ends = count - 1
        head = lax.slice_in_dim(cells, 0, width, axis=dim)
        tail = lax.slice_in_dim(cells, cells.shape[dim] - width, cells.shape[dim], axis=dim)
        cells = jnp.concatenate(
            [
                lax.ppermute(tail, axis, [(i, (i + 1) % count) for i in range(ends)]),
                cells,
                lax.ppermute(head, axis, [((i + 1) % count, i) for i in range(ends)]),
            ],
            axis=dim,
        )
    return cells


def inner_sum(padded):
    total = padded[2:, 1:-1, 1:-1] + padded[:-2, 1:-1, 1:-1]
    total = total + padded[1:-1, 2:, 1:-1] + padded[1:-1, :-2, 1:-1]
    total = total + padded[1:-1, 1:-1, 2:] + padded[1:-1, 1:-1, :-2]
    return total


def operate(field, outer_diag):
    padded = padded_2(field, (("gx", 0), ("gy", 1), ("gz", 2)), 1)
    return (6.0 + outer_diag) * field - inner_sum(padded)


def squares(residual):
    return lax.psum(jnp.sum(residual * residual), ("gx", "gy", "gz"))


def per_device(
    right_side,
    outer_diag,
    stencil_nodes,
    stencil_weights,
    handover_dest,
    handover_cell,
    pressure_prev,
    inner_source,
    inner_diag,
):
    solution_field = jnp.zeros_like(right_side)
    residual = right_side
    direction = right_side
    norm_now = squares(residual)
    for step in range(ITERS):
        image = operate(direction, outer_diag)
        alpha = norm_now / lax.psum(jnp.sum(direction * image), ("gx", "gy", "gz"))
        solution_field = solution_field + alpha * direction
        residual = residual - alpha * image
        norm_next = squares(residual)
        direction = residual + norm_next / norm_now * direction
        norm_now = norm_next
    block_y = right_side.shape[1]
    block_z = right_side.shape[2]
    corner = jnp.arange(stencil_weights.shape[0], dtype=jnp.int32)
    offsets = corner // 4 % 2 * (block_y * block_z) + corner // 2 % 2 * block_z + corner % 2
    nodes = stencil_nodes[None, :] + offsets[:, None]
    sampled = solution_field.reshape(-1)[nodes]
    handed = jnp.sum(stencil_weights * sampled, axis=0)
    across_x = lax.axis_size("gx")
    across_y = lax.axis_size("gy")
    groups = across_x * across_y
    points = handover_dest.shape[0]
    capacity = 2 * points // groups
    dest = handover_dest[:, 0]
    onehot = (dest[None, :] == jnp.arange(groups, dtype=jnp.int32)[:, None]).astype(jnp.int32)
    ranking = jnp.sum(jnp.cumsum(onehot, axis=1) * onehot, axis=0) - 1
    slot_index = dest * capacity + ranking
    rows_out = jnp.stack([handed, handover_cell.astype(jnp.float32)])
    outgoing = jnp.zeros((2, groups * capacity), jnp.float32).at[:, slot_index].set(rows_out)
    incoming = lax.all_to_all(
        outgoing.reshape(2, groups, capacity), ("gx", "gy"), split_axis=1, concat_axis=1, tiled=True
    )
    incoming = incoming.reshape(2, -1)
    cells = incoming[1].astype(jnp.int32)
    rhs = inner_source.reshape(-1).at[cells].add(incoming[0]).reshape(inner_source.shape)
    pressure = pressure_prev
    for sweep in range(SWEEPS):
        padded = padded_2(pressure, (("gx", 0), ("gy", 1), ("gz", 2)), 1)
        pressure = (rhs + inner_sum(padded)) / (6.0 + inner_diag)
    return (solution_field, residual, pressure)


def solution(mesh):
    return jax.shard_map(
        per_device,
        mesh=mesh,
        in_specs=(
            P("gx", "gy", "gz"),
            P("gx", "gy", "gz"),
            P(("gx", "gy", "gz")),
            P(None, ("gx", "gy", "gz")),
            P(("gx", "gy", "gz"), None),
            P(("gx", "gy", "gz")),
            P("gx", "gy", "gz"),
            P("gx", "gy", "gz"),
            P("gx", "gy", "gz"),
        ),
        out_specs=(P("gx", "gy", "gz"), P("gx", "gy", "gz"), P("gx", "gy", "gz")),
        check_vma=False,
    )
```

profile of v0, /device:TPU:1, one launch (start us, length us, event | category | flops | bytes accessed | tf_op | source)
XLA Modules:
  0.0 877.9 jit_solution(10417399929526105254)
XLA Ops:
  0.6 0.7 fusion.48
  1.4 4.9 collective-permute-start.1
  6.3 1.9 collective-permute-start
  8.2 0.8 fusion.42
  9.0 3.6 collective-permute-start.13
  12.7 1.9 collective-permute-start.12
  14.6 0.9 fusion.3
  15.6 2.3 fusion.2
  17.9 34.0 %reduce-window.6 = s32[64,64,128]{2,1,0:T(8,128)S(1)} reduce-window(s32[64,64,128]{2,1,0:T(8,128)} %fusion.2, s32[]{:T(128)} %constant.69.clone.1), window={size=1x1x128 pad=0_0x0_0x127_0}, to_apply=%region_8.9 | reduce-window | flops 66584576 | bytes 4194308 | tf_op jit(solution)/shard_map/reduce-window
  51.9 1.7 slice_reduce_fusion
  53.6 0.2 reduce-window.9
  53.9 0.7 select_reduce_fusion
  54.7 1.3 collective-permute-start.2
  56.0 4.0 collective-permute-start.3
  60.0 0.8 collective-permute-done.3
  60.8 0.1 fusion.44
  60.9 1.3 collective-permute-start.4
  62.2 4.0 collective-permute-start.5
  66.3 1.3 collective-permute-done.4
  67.6 1.7 collective-permute-done.5
  69.3 0.8 multiply_reduce_fusion.3
  70.1 82.9 %all-reduce = (f32[]{:T(128)}, f32[]{:T(128)}) all-reduce(f32[]{:T(128)} %get-tuple-element.4, f32[]{:T(128)} %get-tuple-element.3), channel_id=1, replica_groups=mesh['gx'=16,'gy'=4,'gz'=4] {'gx','gy','gz'}, use_global_device_ids=true, to_apply=%region_1.0 | all-reduce | flops 2 | bytes 16 | tf_op jit(solution)/shard_map/psum | solution.py:40
  154.3 0.6 multiply_reduce_fusion.2
  155.0 0.1 copy.16
  155.1 74.2 %psum.30 = f32[]{:T(128)} all-reduce(f32[]{:T(128)} %multiply_reduce_fusion.2), channel_id=1, replica_groups=mesh['gx'=16,'gy'=4,'gz'=4] {'gx','gy','gz'}, use_global_device_ids=true, to_apply=%region_5.0 | all-reduce | flops 1 | bytes 8 | tf_op jit(solution)/shard_map/psum | solution.py:40
  230.7 2.6 collective-permute-start.6
  233.2 3.0 collective-permute-start.7
  236.3 0.8 collective-permute-done.7
  237.1 1.3 collective-permute-start.8
  238.4 4.0 collective-permute-start.9
  242.4 0.8 collective-permute-done.9
  243.2 0.1 fusion.43
  243.3 1.3 collective-permute-start.10
  244.6 4.0 collective-permute-start.11
  248.7 1.3 collective-permute-start.14
  250.0 4.2 collective-permute-start.15
  254.2 0.8 multiply_reduce_fusion.1
  255.0 76.7 %psum.31 = f32[]{:T(128)} all-reduce(f32[]{:T(128)} %get-tuple-element.7), channel_id=1, replica_groups=mesh['gx'=16,'gy'=4,'gz'=4] {'gx','gy','gz'}, use_global_device_ids=true, to_apply=%region_7.0 | all-reduce | flops 1 | bytes 8 | tf_op jit(solution)/shard_map/psum | solution.py:60
  333.0 0.7 multiply_subtract_fusion
  333.8 362.7 %gather_fusion = f32[65536]{0:T(1024)S(1)} fusion(f32[32768]{0:T(1024)S(1)} %bitcast.20, s32[65536]{0:T(1024)S(1)} %broadcast_clamp_fusion), kind=kCustom, calls=%fused_computation | custom fusion | bytes 786432 | tf_op jit(solution)/shard_map/gather | solution.py:71
  696.6 0.1 multiply_reduce_fusion
  696.8 2.6 copy.14
  699.4 24.5 %scatter_custom_fusion = f32[2,16384]{0,1:T(8,128)} fusion(s32[8192]{0:T(1024)S(1)} %bitcast.35, f32[8192,2]{1,0:T(8,128)} %copy.14, f32[]{:T(128)} %constant.66.clone.1), kind=kCustom, calls=%fused_computation.3 | custom fusion | bytes 131584 | tf_op jit(solution)/shard_map/scatter | solution.py:83
  723.9 5.9 copy.15
  729.8 8.7 all-to-all-start
  738.6 0.1 fusion.39
  738.8 1.3 collective-permute-start.16
  740.1 4.0 collective-permute-start.17
  744.1 4.4 all-to-all-done
  748.5 0.1 fusion.46
  748.7 105.6 %scatter_fusion = f32[65536]{0:T(1024)S(1)} fusion(f32[65536]{0:T(1024)S(1)} %bitcast.21, s32[16384]{0:T(1024)S(1)} %bitcast.27, f32[16384]{0:T(1024)S(1)} %bitcast.28), kind=kCustom, calls=%fused_computation.2 | custom fusion | flops 16384 | bytes 262144 | tf_op jit(solution)/shard_map/scatter-add | solution.py:89
  854.5 0.3 fusion.13
  854.8 2.7 collective-permute-start.18
  857.4 2.9 collective-permute-start.19
  860.4 1.0 collective-permute-done.19
  861.4 1.3 collective-permute-start.20
  862.7 4.9 collective-permute-start.21
  867.6 0.8 collective-permute-done.21
  868.4 0.1 fusion.38
  868.5 1.3 collective-permute-start.22
  869.8 4.0 collective-permute-start.23
  873.8 2.1 collective-permute-done.22
  876.0 0.9 collective-permute-done.23
  876.9 1.0 fusion.6
  (61 shorter events, 0.9 us)
Async XLA Ops:
  1.4 53.2 %collective-permute-start.1 = (f32[1,16,256]{2,1,0:T(8,128)S(1)}, f32[1,16,256]{2,1,0:T(8,128)S(1)}, u32[]{:S(2)}, u32[]{:S(2)}) collective-permute-start(f32[1,16,256]{2,1,0:T(8,128)S(1)} %get-tuple-element.37), channel_id=1, source_target_pairs={{0,16},{16,32},{32,48},{48,64},{64,80},{80,96},{96,112},{112,128},... | collective-permute-start | bytes 49160 | tf_op jit(solution)/shard_map/ppermute | solution.py:18
  6.3 48.4 %collective-permute-start = (f32[1,16,256]{2,1,0:T(8,128)S(1)}, f32[1,16,256]{2,1,0:T(8,128)S(1)}, u32[]{:S(2)}, u32[]{:S(2)}) collective-permute-start(f32[1,16,256]{2,1,0:T(8,128)S(1)} %get-tuple-element.36), channel_id=1, source_target_pairs={{16,0},{32,16},{48,32},{64,48},{80,64},{96,80},{112,96},{128,112},... | collective-permute-start | bytes 49160 | tf_op jit(solution)/shard_map/ppermute | solution.py:20
  9.0 227.2 %collective-permute-start.13 = (f32[1,32,256]{2,1,0:T(8,128)S(1)}, f32[1,32,256]{2,1,0:T(8,128)S(1)}, u32[]{:S(2)}, u32[]{:S(2)}) collective-permute-start(f32[1,32,256]{2,1,0:T(8,128)S(1)} %get-tuple-element.21), channel_id=1, source_target_pairs={{0,16},{16,32},{32,48},{48,64},{64,80},{80,96},{96,112},{112,128},... | collective-permute-start | bytes 98312 | tf_op jit(solution)/shard_map/ppermute | solution.py:18
  12.7 229.8 %collective-permute-start.12 = (f32[1,32,256]{2,1,0:T(8,128)S(1)}, f32[1,32,256]{2,1,0:T(8,128)S(1)}, u32[]{:S(2)}, u32[]{:S(2)}) collective-permute-start(f32[1,32,256]{2,1,0:T(8,128)S(1)} %get-tuple-element.20), channel_id=1, source_target_pairs={{16,0},{32,16},{48,32},{64,48},{80,64},{96,80},{112,96},{128,112},... | collective-permute-start | bytes 98312 | tf_op jit(solution)/shard_map/ppermute | solution.py:20
  51.9 2.0 copy-start.5
  51.9 2.7 copy-start
  53.6 12.7 %copy-start.8 = (s32[8192]{0:T(1024)S(1)}, s32[8192]{0:T(1024)}, u32[]{:S(2)}) copy-start(s32[8192]{0:T(1024)} %param.14) | copy-start | bytes 98308
  53.6 15.7 %copy-start.4 = (f32[8,16,256]{2,1,0:T(8,128)S(1)}, f32[8,16,256]{2,1,0:T(8,128)}, u32[]{:S(2)}) copy-start(f32[8,16,256]{2,1,0:T(8,128)} %param.10) | copy-start | bytes 393220
  53.9 101.1 %copy-start.6 = (f32[8,32,256]{2,1,0:T(8,128)S(1)}, f32[8,32,256]{2,1,0:T(8,128)}, u32[]{:S(2)}) copy-start(f32[8,32,256]{2,1,0:T(8,128)} %param.16) | copy-start | bytes 786436
  54.6 181.7 %copy-start.1 = (f32[8,32,256]{2,1,0:T(8,128)S(1)}, f32[8,32,256]{2,1,0:T(8,128)}, u32[]{:S(2)}) copy-start(f32[8,32,256]{2,1,0:T(8,128)} %param.15) | copy-start | bytes 786436
  54.7 5.3 collective-permute-start.2
  56.0 4.8 collective-permute-start.3
  60.9 6.7 collective-permute-start.4
  62.2 7.1 collective-permute-start.5
  230.7 5.6 collective-permute-start.6
  233.2 3.9 collective-permute-start.7
  237.1 5.3 collective-permute-start.8
  238.4 4.8 collective-permute-start.9
  243.3 10.9 %collective-permute-start.10 = (f32[10,18,1]{2,1,0:T(8,128)S(1)}, f32[10,18,1]{2,1,0:T(8,128)S(1)}, u32[]{:S(2)}, u32[]{:S(2)}) collective-permute-start(f32[10,18,1]{2,1,0:T(8,128)S(1)} %get-tuple-element.22), channel_id=1, source_target_pairs={{1,0},{2,1},{3,2},{5,4},{6,5},{7,6},{9,8},{10,9},{11,10},{13,12},{... | collective-permute-start | bytes 2168 | tf_op jit(solution)/shard_map/ppermute | solution.py:20
  244.6 9.6 %collective-permute-start.11 = (f32[10,18,1]{2,1,0:T(8,128)S(1)}, f32[10,18,1]{2,1,0:T(8,128)S(1)}, u32[]{:S(2)}, u32[]{:S(2)}) collective-permute-start(f32[10,18,1]{2,1,0:T(8,128)S(1)} %get-tuple-element.23), channel_id=1, source_target_pairs={{0,1},{1,2},{2,3},{4,5},{5,6},{6,7},{8,9},{9,10},{10,11},{12,13},{... | collective-permute-start | bytes 2168 | tf_op jit(solution)/shard_map/ppermute | solution.py:18
  248.7 489.9 %collective-permute-start.14 = (f32[10,1,256]{2,1,0:T(1,128)S(1)}, f32[10,1,256]{2,1,0:T(1,128)S(1)}, u32[]{:S(2)}, u32[]{:S(2)}) collective-permute-start(f32[10,1,256]{2,1,0:T(1,128)S(1)} %get-tuple-element.17), channel_id=1, source_target_pairs={{4,0},{8,4},{12,8},{5,1},{9,5},{13,9},{6,2},{10,6},{14,10},{7,3},{... | collective-permute-start | bytes 30728 | tf_op jit(solution)/shard_map/ppermute | solution.py:20
  250.0 488.6 %collective-permute-start.15 = (f32[10,1,256]{2,1,0:T(1,128)S(1)}, f32[10,1,256]{2,1,0:T(1,128)S(1)}, u32[]{:S(2)}, u32[]{:S(2)}) collective-permute-start(f32[10,1,256]{2,1,0:T(1,128)S(1)} %get-tuple-element.16), channel_id=1, source_target_pairs={{0,4},{4,8},{8,12},{1,5},{5,9},{9,13},{2,6},{6,10},{10,14},{3,7},{... | collective-permute-start | bytes 30728 | tf_op jit(solution)/shard_map/ppermute | solution.py:18
  333.7 362.8 %copy-start.3 = (f32[8,16,256]{2,1,0:T(8,128)}, f32[8,16,256]{2,1,0:T(8,128)S(1)}, u32[]{:S(2)}) copy-start(f32[8,16,256]{2,1,0:T(8,128)S(1)} %get-tuple-element.33) | copy-start | bytes 393220
  333.8 362.8 %copy-start.7 = (f32[8,8192]{1,0:T(8,128)S(1)}, f32[8,8192]{1,0:T(8,128)}, u32[]{:S(2)}) copy-start(f32[8,8192]{1,0:T(8,128)} %param.12) | copy-start | bytes 786436
  729.8 18.7 %all-to-all-start = ((f32[2,64,256]{2,0,1:T(2,128)}), f32[2,64,256]{2,0,1:T(2,128)S(1)}, u32[]{:S(2)}, u32[]{:S(2)}) async-start(f32[2,64,256]{2,0,1:T(2,128)} %copy.15), calls=%async_computation | async-start | bytes 262144 | tf_op jit(solution)/shard_map/all_to_all | solution.py:84
  738.8 115.7 %collective-permute-start.16 = (f32[10,34,1]{2,1,0:T(8,128)S(1)}, f32[10,34,1]{2,1,0:T(8,128)S(1)}, u32[]{:S(2)}, u32[]{:S(2)}) collective-permute-start(f32[10,34,1]{2,1,0:T(8,128)S(1)} %get-tuple-element.12), channel_id=1, source_target_pairs={{1,0},{2,1},{3,2},{5,4},{6,5},{7,6},{9,8},{10,9},{11,10},{13,12},{... | collective-permute-start | bytes 4088 | tf_op jit(solution)/shard_map/ppermute | solution.py:20
  740.1 114.4 %collective-permute-start.17 = (f32[10,34,1]{2,1,0:T(8,128)S(1)}, f32[10,34,1]{2,1,0:T(8,128)S(1)}, u32[]{:S(2)}, u32[]{:S(2)}) collective-permute-start(f32[10,34,1]{2,1,0:T(8,128)S(1)} %get-tuple-element.13), channel_id=1, source_target_pairs={{0,1},{1,2},{2,3},{4,5},{5,6},{6,7},{8,9},{9,10},{10,11},{12,13},{... | collective-permute-start | bytes 4088 | tf_op jit(solution)/shard_map/ppermute | solution.py:18
  748.7 105.8 %copy-start.2 = (f32[8,32,256]{2,1,0:T(8,128)S(1)}, f32[8,32,256]{2,1,0:T(8,128)}, u32[]{:S(2)}) copy-start(f32[8,32,256]{2,1,0:T(8,128)} %param.17) | copy-start | bytes 786436
  854.8 5.6 collective-permute-start.18
  857.4 3.9 collective-permute-start.19
  861.4 6.2 collective-permute-start.20
  862.7 5.7 collective-permute-start.21
  868.5 7.4 collective-permute-start.22
  869.8 7.0 collective-permute-start.23
where the time goes:
time: 885 us; the launch traced here: 878 us
  local copies, waits for them, and re-layouts  400 us (45%)
  blocking collectives  234 us (26%)
  other arithmetic  149 us (17%)
  starting transfers between devices  75.7 us (9%)
  waiting for transfers between devices  14.6 us (2%)
    gather x2, local copies, waits for them, and re-layouts, per_device(): sampled = solution_field.reshape(-1)[nodes]  363 us
    psum x2, blocking collectives, squares(): return lax.psum(jnp.sum(residual * residual), ('gx', 'gy', 'gz'))  157 us
    scatter-add x1, other arithmetic, per_device(): inner_source.reshape(-1).at[cells].add(incoming[0])  106 us
    psum x1, blocking collectives, per_device(): alpha = norm_now / lax.psum(jnp.sum(direction * image), ('gx', 'gy', 'gz'))  76.7 us
    ppermute x12, starting transfers between devices, padded_2(): lax.ppermute(tail, axis, [(i, (i + 1) % count) for i in range(ends)])  47.5 us
    another operation x2, other arithmetic  34.2 us
    scatter x1, local copies, waits for them, and re-layouts, per_device(): jnp.zeros((2, groups * capacity), jnp.float32).at[:, slot_index]  24.5 us
    ppermute x12, starting transfers between devices, padded_2(): lax.ppermute(head, axis, [((i + 1) % count, i) for i in range(ends)])  19.4 us
  transfers between devices with their start and end apart: 25, of which 10 were waited for; matrix products, arithmetic and copies ran while one was open for 62% of the time, Pallas kernels for 0%

commit v1 on v0

v1 whole, which is shorter than its diff:
```python
import functools

import jax
import jax.numpy as jnp
from jax import lax
from jax.experimental import pallas as pl
from jax.experimental.pallas import tpu as pltpu
from jax.sharding import PartitionSpec as P

MESH = pl.DeviceIdType.MESH
F32 = jnp.float32
BF16 = jnp.bfloat16
I32 = jnp.int32
LANE = 128
BLK = 256


def iota(shape, dim):
    return lax.broadcasted_iota(I32, shape, dim)


def halves(x):
    hi = x.astype(BF16).astype(F32)
    return hi, x - hi


def nt(a, b):
    return lax.dot_general(a, b, (((1,), (1,)), ((), ())), preferred_element_type=F32)


def nn(a, b):
    return lax.dot_general(a, b, (((1,), (0,)), ((), ())), preferred_element_type=F32)


def two_sum(a, b):
    s = a + b
    t = s - a
    return s, (a - (s - t)) + (b - t)


def two_prod(a, b):
    p = a * b
    ca, cb = 4097.0 * a, 4097.0 * b
    ah, bh = ca - (ca - a), cb - (cb - b)
    al, bl = a - ah, b - bh
    return p, ((ah * bh - p) + ah * bl + al * bh) + al * bl


def dd_times(x, f):
    p, e = two_prod(x[0], f)
    return two_sum(p, e + x[1] * f)


def dd_add(x, y):
    s, e = two_sum(x[0], y[0])
    return two_sum(s, e + (x[1] + y[1]))


def column(v, at):
    groups = v.shape[0] // 8
    tile = at // LANE * LANE
    lanes = v[:, tile : tile + LANE].reshape(groups, 8, LANE)
    spread = jnp.broadcast_to(lanes[:, :, at - tile : at - tile + 1], (groups, 8, LANE))
    keep = iota((groups, 8, LANE), 2) == iota((groups, 8, LANE), 0)
    return jnp.sum(jnp.where(keep, spread, 0.0), axis=0)


def uncolumn(c, rows):
    groups = rows // 8
    keep = iota((groups, 8, LANE), 2) == iota((groups, 8, LANE), 0)
    picked = jnp.where(keep, jnp.broadcast_to(c[None], (groups, 8, LANE)), 0.0)
    return jnp.sum(picked, axis=2, keepdims=True).reshape(rows, 1)


def neighbour_sum(v, halo_x, halo_y, halo_z, at_ends):
    rows, nz = v.shape
    ny = halo_x.shape[1]
    planes = rows // ny
    first_x, last_x, first_y, last_y, first_z, last_z = at_ends
    low = jnp.where(first_x, 0.0, halo_x[0])
    high = jnp.where(last_x, 0.0, halo_x[1])
    total = jnp.concatenate([low, v[: rows - ny]], axis=0)
    total = total + jnp.concatenate([v[ny:], high], axis=0)
    in_plane = iota((rows, nz), 0) % ny

    def rows_of(h):
        return jnp.broadcast_to(h[:, None, :], (planes, ny, nz)).reshape(rows, nz)

    low = rows_of(jnp.where(first_y, 0.0, halo_y[0]))
    high = rows_of(jnp.where(last_y, 0.0, halo_y[1]))
    total = total + jnp.where(in_plane == 0, low, pltpu.roll(v, 1, 0))
    total = total + jnp.where(in_plane == ny - 1, high, pltpu.roll(v, rows - 1, 0))
    lane = iota((rows, nz), 1)
    low = uncolumn(jnp.where(first_z, 0.0, halo_z[0]), rows)
    high = uncolumn(jnp.where(last_z, 0.0, halo_z[1]), rows)
    total = total + jnp.where(lane == 0, low, pltpu.roll(v, 1, 1))
    total = total + jnp.where(lane == nz - 1, high, pltpu.roll(v, nz - 1, 1))
    return total


def kernel(
    sizes,
    right_hbm, odiag_hbm, nodes_hbm, weights_hbm, dest_hbm, cell_hbm, prev_hbm, source_hbm, idiag_hbm,
    x_hbm, res_hbm, p_hbm,
    right, odiag, nodes, weights, dest, cell, prev, source, idiag, load_sem,
    q0, q1, p1, x_out, res_out, p_out, store_sem,
    hx_o, hy_o, hz_o, sy_o, sz_o, hx_i, hy_i, hz_i, sy_i, sz_i, halo_send, halo_recv,
    ar1, ar2, ar_send, ar_recv,
    tx, rx, tx_cells, rx_cells, a2a_send, a2a_recv,
    rank_hot, dest_hot, carry, cells_acc, col_hot, row_weight, handed,
    cell_row, cell_col, acc,
):
    ngx, ngy, ngz, cy, iy = sizes
    mx, my, mz = lax.axis_index("gx"), lax.axis_index("gy"), lax.axis_index("gz")
    groups = ngx * ngy
    me = mx * ngy + my
    points = nodes.shape[1]
    blocks = points // BLK
    cap = tx.shape[2]
    at_ends = (mx == 0, mx == ngx - 1, my == 0, my == ngy - 1, mz == 0, mz == ngz - 1)

    loads = []
    for i, (a, b) in enumerate(
        ((right_hbm, right), (dest_hbm, dest), (cell_hbm, cell), (odiag_hbm, odiag), (prev_hbm, prev),
         (nodes_hbm, nodes), (weights_hbm, weights), (source_hbm, source), (idiag_hbm, idiag))
    ):
        c = pltpu.make_async_copy(a, b, load_sem.at[i])
        c.start()
        loads.append(c)

    barrier = pltpu.get_barrier_semaphore()

    def peer(k):
        t = lax.rem(me + k, groups)
        return t, (t // ngy, lax.rem(t, ngy), mz)

    def side(k):
        t = lax.rem(my * ngz + mz + k, ngy * ngz)
        return t, (mx, t // ngz, lax.rem(t, ngz))

    def greet_peer(k, _):
        pl.semaphore_signal(barrier, inc=1, device_id=peer(k)[1], device_id_type=MESH)
        return 0

    lax.fori_loop(1, groups, greet_peer, 0)

    def greet_layer(k, _):
        z = lax.rem(mz + 1 + k // ngy, ngz)
        pl.semaphore_signal(barrier, inc=1, device_id=(mx, lax.rem(k, ngy), z), device_id_type=MESH)
        return 0

    lax.fori_loop(0, (ngz - 1) * ngy, greet_layer, 0)
    for c in loads[:1]:
        c.wait()
    pl.semaphore_wait(barrier, groups - 1 + (ngz - 1) * ngy)

    up = ((lax.rem(mx + 1, ngx), my, mz), (mx, lax.rem(my + 1, ngy), mz), (mx, my, lax.rem(mz + 1, ngz)))
    down = (
        (lax.rem(mx + ngx - 1, ngx), my, mz),
        (mx, lax.rem(my + ngy - 1, ngy), mz),
        (mx, my, lax.rem(mz + ngz - 1, ngz)),
    )

    def send_halo(which, src, hx, hy, hz, sy, sz, slot):
        rows, nz = src.shape
        ny = hx.shape[2]
        planes = rows // ny
        copies = []

        def send(j, a, b, to):
            c = pltpu.make_async_remote_copy(
                a, b, halo_send.at[which, j], halo_recv.at[which, j], device_id=to, device_id_type=MESH
            )
            c.start()
            copies.append(c)

        send(0, src.at[pl.ds(rows - ny, ny)], hx.at[slot, 0], up[0])
        send(1, src.at[pl.ds(0, ny)], hx.at[slot, 1], down[0])
        v = src[...]
        solid = v.reshape(planes, ny, nz)
        sy[slot, 0] = solid[:, ny - 1, :]
        sy[slot, 1] = solid[:, 0, :]
        send(2, sy.at[slot, 0], hy.at[slot, 0], up[1])
        send(3, sy.at[slot, 1], hy.at[slot, 1], down[1])
        sz[slot, 0] = column(v, nz - 1)
        sz[slot, 1] = column(v, 0)
        send(4, sz.at[slot, 0], hz.at[slot, 0], up[2])
        send(5, sz.at[slot, 1], hz.at[slot, 1], down[2])
        return copies

    outer = (hx_o, hy_o, hz_o, sy_o, sz_o)
    inner = (hx_i, hy_i, hz_i, sy_i, sz_i)
    unsent = []
    first = send_halo(0, right, *outer, 0)
    loads[4].wait()
    prev_halo = send_halo(1, prev, *inner, 0)

    loads[1].wait()
    loads[2].wait()
    tri = jnp.concatenate(
        [
            jnp.where(iota((BLK, BLK), 0) < iota((BLK, BLK), 1), 1.0, 0.0),
            jnp.ones((BLK, BLK), F32),
        ],
        axis=1,
    ).astype(BF16)
    carry[...] = jnp.zeros_like(carry)
    step = 8 if blocks % 8 == 0 else 1
    group_id = iota((groups, BLK), 0)
    slot_id = iota((cap, BLK), 0).astype(F32)

    def rank_step(j, _):
        base = pl.multiple_of(j * step * BLK, BLK)
        names = dest[:, pl.ds(base, step * BLK)]
        hots = [
            jnp.where(group_id == names[:, b * BLK : (b + 1) * BLK], 1.0, 0.0)
            for b in range(step)
        ]
        counts = nn(jnp.concatenate(hots, axis=0).astype(BF16), tri)
        seen = carry[...]
        for b in range(step):
            part = counts[b * groups : (b + 1) * groups]
            rank = jnp.sum(hots[b] * (part[:, :BLK] + seen), axis=0, keepdims=True)
            seen = seen + part[:, BLK:]
            at = pl.ds(pl.multiple_of(base + b * BLK, BLK), BLK)
            rank_hot[:, at] = jnp.where(slot_id == rank, 1.0, 0.0).astype(BF16)
            dest_hot[:, at] = hots[b].astype(BF16)
        carry[...] = seen
        return 0

    lax.fori_loop(0, blocks // step, rank_step, 0)

    wide = min(points, 2048)

    cells_acc[...] = jnp.zeros_like(cells_acc)

    def cells_step(j, _):
        at = pl.ds(pl.multiple_of(j * wide, wide), wide)
        c = cell[:, at]
        hot = dest_hot[:, at].astype(F32)
        left = jnp.concatenate([hot * (c // 256).astype(F32), hot * (c % 256).astype(F32)], axis=0).astype(BF16)
        cells_acc[...] += nt(left, rank_hot[:, at])
        return 0

    lax.fori_loop(0, points // wide, cells_step, 0)
    both = cells_acc[...]
    tx_cells[...] = (both[:groups] * 256.0 + both[groups:]).astype(I32).reshape(groups, 1, cap)

    def exchange(src, dst, which):
        def go(k, _):
            t, to = peer(k)
            pltpu.make_async_remote_copy(
                src.at[t], dst.at[me], a2a_send.at[which], a2a_recv.at[which], device_id=to, device_id_type=MESH
            ).start()
            return 0

        lax.fori_loop(1, groups, go, 0)
        dst[pl.ds(me, 1)] = src[pl.ds(me, 1)]

    def exchanged(src, dst, which):
        many = pl.ds(0, groups - 1)
        pltpu.make_async_copy(dst.at[many], dst.at[many], a2a_recv.at[which]).wait()

    def exchange_sent(src, dst, which):
        many = pl.ds(0, groups - 1)
        pltpu.make_async_copy(src.at[many], src.at[many], a2a_send.at[which]).wait()

    exchange(tx_cells, rx_cells, 0)

    for c in first:
        c.wait_recv()
    loads[3].wait()
    r = right[...]
    diag = 6.0 + odiag[...]
    q0[...] = diag * r - neighbour_sum(r, hx_o[0], hy_o[0], hz_o[0], at_ends)
    second = send_halo(2, q0, *outer, 1)

    loads[5].wait()
    loads[6].wait()
    nz = right.shape[1]
    row_id = iota((right.shape[0], BLK), 0)
    col_id = iota((nz, BLK), 0)

    def weigh(j, _):
        at = pl.ds(pl.multiple_of(j * BLK, BLK), BLK)
        n = nodes[:, at]
        off = row_id - n // nz
        w = weights[:, at]
        hits = (off == 0, off == 1, off == cy, off == cy + 1)
        for dc in range(2):
            total = jnp.zeros(off.shape, F32)
            for hit, k in zip(hits, (0, 2, 4, 6)):
                total = jnp.where(hit, w[k + dc : k + dc + 1], total)
            row_weight[pl.ds(dc * off.shape[0], off.shape[0]), at] = total
        col_hot[:, at] = jnp.where(col_id == n % nz, 1.0, 0.0).astype(BF16)
        return 0

    lax.fori_loop(0, blocks // 2, weigh, 0)

    for c in second:
        c.wait_recv()
    q = q0[...]
    qq = diag * q - neighbour_sum(q, hx_o[1], hy_o[1], hz_o[1], at_ends)
    q1[...] = qq
    row8 = iota((8, LANE), 0)
    packed = jnp.zeros((8, LANE), F32)
    for k, (a, b) in enumerate(((r, r), (r, q), (q, q), (q, qq))):
        s = jnp.sum((a * b).reshape(-1, 8, nz), axis=0)
        t = s[:, :LANE]
        for m in range(LANE, nz, LANE):
            t = t + s[:, m : m + LANE]
        packed = jnp.where(row8 == k, jnp.sum(t, axis=0, keepdims=True), packed)
    packed = jnp.broadcast_to(jnp.sum(packed, axis=1, keepdims=True), (8, LANE))

    def all_to_one(value, buf, n, mine, partner, which):
        buf[pl.ds(mine, 1)] = value[None]

        def go(k, _):
            pltpu.make_async_remote_copy(
                buf.at[mine], buf.at[mine], ar_send.at[which], ar_recv.at[which],
                device_id=partner(k), device_id_type=MESH,
            ).start()
            return 0

        lax.fori_loop(1, n, go, 0)

    def all_arrived(buf, n, which):
        many = pl.ds(0, n - 1)
        pltpu.make_async_copy(buf.at[many], buf.at[many], ar_recv.at[which]).wait()
        s, e = buf[0], jnp.zeros((8, LANE), F32)
        for i in range(1, n):
            s, d = two_sum(s, buf[i])
            e = e + d
        return s + jnp.where(row8 >= 4, pltpu.roll(e, 4, 0), 0.0)

    def all_sent(buf, n, which):
        many = pl.ds(0, n - 1)
        pltpu.make_async_copy(buf.at[many], buf.at[many], ar_send.at[which]).wait()

    all_to_one(packed, ar1, ngx, mx, lambda k: (lax.rem(mx + k, ngx), my, mz), 0)
    lax.fori_loop(blocks // 2, blocks, weigh, 0)
    packed = all_arrived(ar1, ngx, 0)
    all_to_one(packed, ar2, ngy * ngz, my * ngz + mz, lambda k: side(k)[1], 1)

    for c in prev_halo:
        c.wait_recv()
    loads[7].wait()
    loads[8].wait()
    p1[...] = source[...] + neighbour_sum(prev[...], hx_i[0], hy_i[0], hz_i[0], at_ends)
    exchanged(tx_cells, rx_cells, 0)
    nzi = source.shape[1]
    in_row = iota((source.shape[0], cap), 0)
    in_col = iota((nzi, cap), 0)

    def place(s, _):
        c = rx_cells[s]
        at = pl.ds(pl.multiple_of(s * cap, LANE), cap)
        cell_row[:, at] = jnp.where(in_row == c // nzi, 1.0, 0.0).astype(BF16)
        cell_col[:, at] = jnp.where(in_col == c % nzi, 1.0, 0.0).astype(BF16)
        return 0

    lax.fori_loop(0, groups // 2, place, 0)

    mu_rows = all_arrived(ar2, ngy * ngz, 1)
    mu = [(mu_rows[k : k + 1], mu_rows[4 + k : 5 + k]) for k in range(4)]
    a0 = mu[0][0] / mu[1][0]
    two_a0 = 2.0 * a0
    rr1 = dd_add(mu[0], dd_times(dd_add(dd_times(mu[2], a0), (-2.0 * mu[1][0], -2.0 * mu[1][1])), a0))
    rr1 = rr1[0] + rr1[1]
    beta = rr1 / mu[0][0]
    g = 1.0 + beta
    m2 = dd_times(mu[2], -two_a0)
    curve = dd_times(dd_add(dd_times(mu[1], g), m2), g)
    curve = dd_add(curve, dd_times(dd_times(mu[3], a0), a0))
    a1 = rr1 / (curve[0] + curve[1])
    a0, a1, beta = a0[:, :1], a1[:, :1], beta[:, :1]
    r = right[...]
    q = q0[...]
    r1 = r - a0 * q
    d1 = r1 + beta * r
    x = a0 * r + a1 * d1
    x_out[...] = x
    res_out[...] = r1 - a1 * ((q - a0 * q1[...]) + beta * q)
    stores = [
        pltpu.make_async_copy(x_out, x_hbm, store_sem.at[0]),
        pltpu.make_async_copy(res_out, res_hbm, store_sem.at[1]),
    ]
    for c in stores:
        c.start()

    nr = x.shape[0]
    ahead = pltpu.roll(x, nz - 1, 1)
    ahead = jnp.where(iota((nr, nz), 1) == nz - 1, pltpu.roll(ahead, nr - 1, 0), ahead)
    field = jnp.concatenate([x, ahead], axis=0)
    hi, lo = halves(field)
    field = jnp.concatenate([hi, lo], axis=0).astype(BF16)
    mid = 4 if blocks % 4 == 0 else 1

    def sample(j, _):
        for b in range(mid):
            at = pl.ds(pl.multiple_of((j * mid + b) * BLK, BLK), BLK)
            got = nn(field, col_hot[:, at])
            got = (got[: 2 * nr] + got[2 * nr :]) * row_weight[:, at]
            handed[:, at] = jnp.sum(got, axis=0, keepdims=True)
        return 0

    lax.fori_loop(0, blocks // mid, sample, 0)

    acc[pl.ds(0, 2 * groups)] = jnp.zeros((2 * groups, cap), F32)

    def route(j, _):
        at = pl.ds(pl.multiple_of(j * wide, wide), wide)
        h_hi, h_lo = halves(handed[:, at])
        hot = dest_hot[:, at].astype(F32)
        left = jnp.concatenate([hot * h_hi, hot * h_lo], axis=0).astype(BF16)
        acc[pl.ds(0, 2 * groups)] += nt(left, rank_hot[:, at])
        return 0

    lax.fori_loop(0, points // wide, route, 0)
    tx[...] = (acc[pl.ds(0, groups)] + acc[pl.ds(groups, groups)]).reshape(groups, 1, cap)
    exchange(tx, rx, 1)
    lax.fori_loop(groups // 2, groups, place, 0)
    acc[...] = jnp.zeros_like(acc)
    inv = 1.0 / (6.0 + idiag[...])
    exchanged(tx, rx, 1)

    ni = source.shape[0]
    batch = 8 if groups % 8 == 0 else groups

    def gather_in(j, _):
        at = pl.ds(pl.multiple_of(j * batch * cap, LANE), batch * cap)
        val = jnp.concatenate([rx[j * batch + b] for b in range(batch)], axis=1)
        v_hi, v_lo = halves(val)
        rows = cell_row[:, at]
        left = jnp.concatenate([rows * v_hi.astype(BF16), rows * v_lo.astype(BF16)], axis=0)
        acc[...] += nt(left, cell_col[:, at])
        return 0

    lax.fori_loop(0, groups // batch, gather_in, 0)
    added = acc[pl.ds(0, ni)] + acc[pl.ds(ni, ni)]
    p = (p1[...] + added) * inv
    p1[...] = p
    last = send_halo(3, p1, *inner, 1)
    rhs = source[...] + added
    for c in last:
        c.wait_recv()
    p_out[...] = (rhs + neighbour_sum(p, hx_i[1], hy_i[1], hz_i[1], at_ends)) * inv
    c = pltpu.make_async_copy(p_out, p_hbm, store_sem.at[2])
    c.start()
    stores.append(c)
    for c in first + prev_halo + second + last:
        c.wait_send()
    exchange_sent(tx_cells, rx_cells, 0)
    exchange_sent(tx, rx, 1)
    all_sent(ar1, ngx, 0)
    all_sent(ar2, ngy * ngz, 1)
    for c in stores:
        c.wait()


def solution(mesh):
    ngx, ngy, ngz = (mesh.shape[a] for a in ("gx", "gy", "gz"))
    groups = ngx * ngy

    def per_device(right, odiag, nodes, weights, dest, cell, prev, source, idiag):
        cx, cy, nz = right.shape
        ix, iy, nzi = source.shape
        points = nodes.shape[0]
        cap = 2 * points // groups
        no, ni = cx * cy, ix * iy
        v = pltpu.VMEM
        dma = pltpu.SemaphoreType.DMA
        scratch = [
            v((no, nz), F32), v((no, nz), F32), v((1, points), I32), v((8, points), F32), v((1, points), I32),
            v((1, points), I32), v((ni, nzi), F32), v((ni, nzi), F32), v((ni, nzi), F32), dma((9,)),
            v((no, nz), F32), v((no, nz), F32), v((ni, nzi), F32), v((no, nz), F32), v((no, nz), F32), v((ni, nzi), F32), dma((3,)),
            v((2, 2, cy, nz), F32), v((2, 2, cx, nz), F32), v((2, 2, 8, LANE), F32), v((2, 2, cx, nz), F32), v((2, 2, 8, LANE), F32),
            v((2, 2, iy, nzi), F32), v((2, 2, ix, nzi), F32), v((2, 2, 8, LANE), F32), v((2, 2, ix, nzi), F32), v((2, 2, 8, LANE), F32),
            dma((4, 6)), dma((4, 6)),
            v((ngx, 8, LANE), F32), v((ngy * ngz, 8, LANE), F32), dma((2,)), dma((2,)),
            v((groups, 1, cap), F32), v((groups, 1, cap), F32), v((groups, 1, cap), I32), v((groups, 1, cap), I32), dma((2,)), dma((2,)),
            v((cap, points), BF16), v((groups, points), BF16), v((groups, BLK), F32), v((2 * groups, cap), F32),
            v((nz, points), BF16), v((2 * no, points), F32), v((1, points), F32),
            v((ni, groups * cap), BF16), v((nzi, groups * cap), BF16), v((2 * ni, nzi), F32),
        ]
        x, res, p = pl.pallas_call(
            functools.partial(kernel, (ngx, ngy, ngz, cy, iy)),
            out_shape=(
                jax.ShapeDtypeStruct((no, nz), F32),
                jax.ShapeDtypeStruct((no, nz), F32),
                jax.ShapeDtypeStruct((ni, nzi), F32),
            ),
            in_specs=[pl.BlockSpec(memory_space=pl.ANY)] * 9,
            out_specs=[pl.BlockSpec(memory_space=pl.ANY)] * 3,
            scratch_shapes=scratch,
            compiler_params=pltpu.CompilerParams(
                collective_id=0, has_side_effects=True, vmem_limit_bytes=56 * 2**20
            ),
        )(
            right.reshape(no, nz), odiag.reshape(no, nz), nodes.reshape(1, points), weights,
            dest.reshape(1, points), cell.reshape(1, points), prev.reshape(ni, nzi),
            source.reshape(ni, nzi), idiag.reshape(ni, nzi),
        )
        return x.reshape(cx, cy, nz), res.reshape(cx, cy, nz), p.reshape(ix, iy, nzi)

    block = P("gx", "gy", "gz")
    every = ("gx", "gy", "gz")
    return jax.shard_map(
        per_device,
        mesh=mesh,
        in_specs=(block, block, P(every), P(None, every), P(every, None), P(every), block, block, block),
        out_specs=(block, block, block),
        check_vma=False,
    )
```

time: 885 us -> 58.6 us (0.07)
  local copies, waits for them, and re-layouts: 400 us -> 2.98 us
  blocking collectives: 234 us -> 0 us
  other arithmetic: 149 us -> 0 us
  starting transfers between devices: 75.7 us -> 0 us
  Pallas kernels: 0 us -> 54.9 us
  waiting for transfers between devices: 14.6 us -> 0 us
    gather x2 -> x0, local copies, waits for them, and re-layouts: 363 us -> none  [per_device(): sampled = solution_field.reshape(-1)[nodes]]
    psum x3 -> x0, blocking collectives: 234 us -> none  [the longest x2 157 us: squares(): return lax.psum(jnp.sum(residual * residual), ('gx', 'gy', 'gz'))]
    scatter-add x1 -> x0, other arithmetic: 106 us -> none  [per_device(): inner_source.reshape(-1).at[cells].add(incoming[0])]
    ppermute x24 -> x0, starting transfers between devices: 66.9 us -> none  [the longest x12 47.5 us: padded_2(): lax.ppermute(tail, axis, [(i, (i + 1) % count) for i in range(ends)])]
    pallas_call x0 -> x1, Pallas kernels: none -> 54.9 us  [per_device(): pl.pallas_call(functools.partial(kernel, (ngx, ngy, ngz, cy, iy)), out_sh...]
    another operation x3 -> x0, other arithmetic: 34.3 us -> none
    scatter x1 -> x0, local copies, waits for them, and re-layouts: 24.5 us -> none  [per_device(): jnp.zeros((2, groups * capacity), jnp.float32).at[:, slot_index]]
    ppermute x24 -> x0, waiting for transfers between devices: 10.2 us -> none  [the longest x12 6.68 us: padded_2(): lax.ppermute(tail, axis, [(i, (i + 1) % count) for i in range(ends)])]
  transfers between devices with their start and end apart: 25 -> 0, of which waited for: 10 -> 0; matrix products, arithmetic and copies ran while one was open for 62% -> 0% of each run, Pallas kernels for 0% -> 0%
where the time goes in v1:
time: 58.6 us; the launch traced here: 58.5 us
  Pallas kernels  54.9 us (94%)
  local copies, waits for them, and re-layouts  2.98 us (5%)
  between operations  0.66 us (1%)
    pallas_call x1, Pallas kernels, per_device(): pl.pallas_call(functools.partial(kernel, (ngx, ngy, ngz, cy, iy)), out_sh...  54.9 us
    unnamed x7, local copies, waits for them, and re-layouts  2.98 us

profile of v1, /device:TPU:1, one launch (start us, length us, event | category | flops | bytes accessed | tf_op | source)
XLA Modules:
  0.0 58.5 jit_solution(988998146094098560)
XLA Ops:
  0.6 54.9 %shard_map.112 = (f32[128,256]{1,0:T(8,128)}, f32[128,256]{1,0:T(8,128)}, f32[256,256]{1,0:T(8,128)}) custom-call(f32[128,256]{1,0:T(8,128)} %bitcast.17, f32[128,256]{1,0:T(8,128)} %bitcast.18, s32[1,8192]{1,0:T(1,128)} %bitcast.19, f32[8,8192]{1,0:T(8,128)} %weights_hbm.1, s32[1,8192]{1,0:T(1,128)} %bitcast.20, s32[1,8192]{1,0:T(1,128)} %bitcast.21, ...), custom_call_target="tpu_custom_call" | custom-call | tf_op jit(solution)/shard_map/pallas_call | solution.py:486
  55.5 0.0 copy-start.1
  55.5 0.0 copy-start
  55.5 1.6 %copy.15 = f32[8,16,256]{2,1,0:T(8,128)} copy(f32[8,16,256]{2,1,0:T(8,128)} %bitcast.16) | data formatting | bytes 262144
  57.2 0.0 copy-done.1
  57.2 0.7 %copy.16 = f32[8,16,256]{2,1,0:T(8,128)} copy(f32[8,16,256]{2,1,0:T(8,128)S(1)} %bitcast.15) | data formatting | bytes 262144
  57.8 0.0 copy-done
  57.8 0.7 %copy.17 = f32[8,32,256]{2,1,0:T(8,128)} copy(f32[8,32,256]{2,1,0:T(8,128)S(1)} %bitcast.11) | data formatting | bytes 524288
Async XLA Ops:
  55.5 1.6 %copy-start.1 = (f32[128,256]{1,0:T(8,128)S(1)}, f32[128,256]{1,0:T(8,128)}, u32[]{:S(2)}) copy-start(f32[128,256]{1,0:T(8,128)} %get-tuple-element.7) | copy-start | bytes 393220
  55.5 2.3 %copy-start = (f32[256,256]{1,0:T(8,128)S(1)}, f32[256,256]{1,0:T(8,128)}, u32[]{:S(2)}) copy-start(f32[256,256]{1,0:T(8,128)} %get-tuple-element.8) | copy-start | bytes 786436

commit v2 on v1

v2 whole, which is shorter than its diff:
```python
import functools

import jax
import jax.numpy as jnp
from jax import lax
from jax.experimental import pallas as pl
from jax.experimental.pallas import tpu as pltpu
from jax.sharding import PartitionSpec as P

MESH = pl.DeviceIdType.MESH
F32 = jnp.float32
BF16 = jnp.bfloat16
I32 = jnp.int32
LANE = 128
BLK = 256


def iota(shape, dim):
    return lax.broadcasted_iota(I32, shape, dim)


def halves(x):
    hi = x.astype(BF16).astype(F32)
    return hi, x - hi


def nt(a, b):
    return lax.dot_general(a, b, (((1,), (1,)), ((), ())), preferred_element_type=F32)


def nn(a, b):
    return lax.dot_general(a, b, (((1,), (0,)), ((), ())), preferred_element_type=F32)


def two_sum(a, b):
    s = a + b
    t = s - a
    return s, (a - (s - t)) + (b - t)


def two_prod(a, b):
    p = a * b
    ca, cb = 4097.0 * a, 4097.0 * b
    ah, bh = ca - (ca - a), cb - (cb - b)
    al, bl = a - ah, b - bh
    return p, ((ah * bh - p) + ah * bl + al * bh) + al * bl


def dd_times(x, f):
    p, e = two_prod(x[0], f)
    return two_sum(p, e + x[1] * f)


def dd_add(x, y):
    s, e = two_sum(x[0], y[0])
    return two_sum(s, e + (x[1] + y[1]))


def column(v, at):
    groups = v.shape[0] // 8
    tile = at // LANE * LANE
    lanes = v[:, tile : tile + LANE].reshape(groups, 8, LANE)
    spread = jnp.broadcast_to(lanes[:, :, at - tile : at - tile + 1], (groups, 8, LANE))
    keep = iota((groups, 8, LANE), 2) == iota((groups, 8, LANE), 0)
    return jnp.sum(jnp.where(keep, spread, 0.0), axis=0)


def uncolumn(c, rows):
    groups = rows // 8
    keep = iota((groups, 8, LANE), 2) == iota((groups, 8, LANE), 0)
    picked = jnp.where(keep, jnp.broadcast_to(c[None], (groups, 8, LANE)), 0.0)
    return jnp.sum(picked, axis=2, keepdims=True).reshape(rows, 1)


def near_sum(v, ny):
    rows, nz = v.shape
    zero = jnp.zeros((ny, nz), F32)
    total = jnp.concatenate([zero, v[: rows - ny]], axis=0) + jnp.concatenate([v[ny:], zero], axis=0)
    in_plane = iota((rows, nz), 0) % ny
    lane = iota((rows, nz), 1)
    total = total + jnp.where(in_plane == 0, 0.0, pltpu.roll(v, 1, 0))
    total = total + jnp.where(in_plane == ny - 1, 0.0, pltpu.roll(v, rows - 1, 0))
    total = total + jnp.where(lane == 0, 0.0, pltpu.roll(v, 1, 1))
    return total + jnp.where(lane == nz - 1, 0.0, pltpu.roll(v, nz - 1, 1))


def far_sum(shape, halo_x, halo_y, halo_z, at_ends):
    rows, nz = shape
    ny = halo_x.shape[1]
    planes = rows // ny
    first_x, last_x, first_y, last_y, first_z, last_z = at_ends
    low = jnp.where(first_x, 0.0, halo_x[0])
    high = jnp.where(last_x, 0.0, halo_x[1])
    total = jnp.concatenate([low, jnp.zeros((rows - 2 * ny, nz), F32), high], axis=0)
    in_plane = iota((rows, nz), 0) % ny
    lane = iota((rows, nz), 1)

    def rows_of(h):
        return jnp.broadcast_to(h[:, None, :], (planes, ny, nz)).reshape(rows, nz)

    total = total + jnp.where(in_plane == 0, rows_of(jnp.where(first_y, 0.0, halo_y[0])), 0.0)
    total = total + jnp.where(in_plane == ny - 1, rows_of(jnp.where(last_y, 0.0, halo_y[1])), 0.0)
    total = total + jnp.where(lane == 0, uncolumn(jnp.where(first_z, 0.0, halo_z[0]), rows), 0.0)
    return total + jnp.where(lane == nz - 1, uncolumn(jnp.where(last_z, 0.0, halo_z[1]), rows), 0.0)


def field_of(x):
    nr, nz = x.shape
    ahead = pltpu.roll(x, nz - 1, 1)
    ahead = jnp.where(iota((nr, nz), 1) == nz - 1, pltpu.roll(ahead, nr - 1, 0), ahead)
    hi, lo = halves(jnp.concatenate([x, ahead], axis=0))
    return jnp.concatenate([hi, lo], axis=0).astype(BF16)


def hot_bf16(ids, wanted, value):
    return jnp.where(ids == wanted.astype(BF16), jnp.broadcast_to(value.astype(BF16), ids.shape), jnp.zeros(ids.shape, BF16))


def interpolate(field, n, w, cy, nz):
    nr = field.shape[0] // 4
    planes, parts, blk = nr // cy, cy // 8, n.shape[1]
    row = n // nz
    a0 = jnp.broadcast_to(row // cy, (8, blk))
    b0 = jnp.broadcast_to(row % cy, (8, blk))
    column_hot = hot_bf16(iota((nz, blk), 0).astype(BF16), n % nz, jnp.ones((1, blk), F32))
    got = nn(field, column_hot)
    got = got[: 2 * nr] + got[2 * nr :]
    here = [a0 == a for a in range(planes - 1)]

    def pick(dc, part, ahead):
        def at(a):
            s = dc * nr + min(a + ahead, planes - 1) * cy + part * 8
            return got[s : s + 8]

        v = at(planes - 2)
        for a in range(planes - 3, -1, -1):
            v = jnp.where(here[a], at(a), v)
        return v

    sub = iota((8, blk), 0)
    total = jnp.zeros((8, blk), F32)
    for dc in range(2):
        picked = [[pick(dc, part, ahead) for part in range(parts)] for ahead in range(2)] + [[pick(dc, 0, 2)]]
        for da in range(2):
            wa, wb = w(da * 4 + dc), w(da * 4 + 2 + dc)
            for part in range(parts):
                wt = jnp.where(b0 == sub + 8 * part, wa, jnp.where(b0 + 1 == sub + 8 * part, wb, 0.0))
                total = total + wt * picked[da][part]
            total = total + jnp.where(b0 + 1 == sub + cy, wb, 0.0) * picked[da + 1][0]
    return jnp.sum(total, axis=0, keepdims=True)


def kernel(
    sizes,
    right_hbm, odiag_hbm, nodes_hbm, weights_hbm, dest_hbm, cell_hbm, prev_hbm, source_hbm, idiag_hbm,
    x_hbm, res_hbm, p_hbm,
    right, odiag, nodes, weights, dest, cell, prev, source, idiag, load_sem,
    q0, q1, p1, x_out, res_out, p_out, store_sem,
    hx_o, hy_o, hz_o, sy_o, sz_o, hx_i, hy_i, hz_i, sy_i, sz_i, halo_send, halo_recv,
    ar1, ar2, ar_send, ar_recv,
    tx, rx, a2a_send, a2a_recv,
    rank, carry, field, handed_r, handed_q, routed, acc, inv,
):
    ngx, ngy, ngz, cy, iy = sizes
    mx, my, mz = lax.axis_index("gx"), lax.axis_index("gy"), lax.axis_index("gz")
    groups = ngx * ngy
    me = mx * ngy + my
    points = nodes.shape[1]
    blocks = points // BLK
    cap = tx.shape[2] // 3
    at_ends = (mx == 0, mx == ngx - 1, my == 0, my == ngy - 1, mz == 0, mz == ngz - 1)

    barrier = pltpu.get_barrier_semaphore()

    def peer(k):
        t = lax.rem(me + k, groups)
        return t, (t // ngy, lax.rem(t, ngy), mz)

    def greet_peer(k, _):
        pl.semaphore_signal(barrier, inc=1, device_id=peer(k)[1], device_id_type=MESH)
        return 0

    loads = []
    for i, (a, b) in enumerate(
        ((right_hbm, right), (dest_hbm, dest), (nodes_hbm, nodes), (weights_hbm, weights), (odiag_hbm, odiag),
         (cell_hbm, cell), (prev_hbm, prev), (source_hbm, source), (idiag_hbm, idiag))
    ):
        c = pltpu.make_async_copy(a, b, load_sem.at[i])
        c.start()
        loads.append(c)
    lax.fori_loop(1, groups, greet_peer, 0)
    side = [(a, b) for a in range(ngy) for b in range(ngz) if (a, b) != (0, 0)]
    side.sort(key=lambda t: -(min(t[0], ngy - t[0]) + min(t[1], ngz - t[1])))
    along = sorted(range(1, ngx), key=lambda k: -min(k, ngx - k))

    def beside(a, b):
        return (mx, lax.rem(my + a, ngy), lax.rem(mz + b, ngz))

    others = [(a, b) for a, b in side if b]
    for a, b in others:
        pl.semaphore_signal(barrier, inc=1, device_id=beside(a, b), device_id_type=MESH)

    up = ((lax.rem(mx + 1, ngx), my, mz), (mx, lax.rem(my + 1, ngy), mz), (mx, my, lax.rem(mz + 1, ngz)))
    down = (
        (lax.rem(mx + ngx - 1, ngx), my, mz),
        (mx, lax.rem(my + ngy - 1, ngy), mz),
        (mx, my, lax.rem(mz + ngz - 1, ngz)),
    )

    def pack_halo(src, sy, sz, ny, slot):
        rows, nz = src.shape
        v = src[...]
        solid = v.reshape(rows // ny, ny, nz)
        sy[slot, 0] = solid[:, ny - 1, :]
        sy[slot, 1] = solid[:, 0, :]
        sz[slot, 0] = column(v, nz - 1)
        sz[slot, 1] = column(v, 0)

    def send_halo(which, src, hx, hy, hz, sy, sz, slot):
        rows = src.shape[0]
        ny = hx.shape[2]
        copies = []

        def send(j, a, b, to):
            c = pltpu.make_async_remote_copy(
                a, b, halo_send.at[which, j], halo_recv.at[which, j], device_id=to, device_id_type=MESH
            )
            c.start()
            copies.append(c)

        send(0, src.at[pl.ds(rows - ny, ny)], hx.at[slot, 0], up[0])
        send(1, src.at[pl.ds(0, ny)], hx.at[slot, 1], down[0])
        send(2, sy.at[slot, 0], hy.at[slot, 0], up[1])
        send(3, sy.at[slot, 1], hy.at[slot, 1], down[1])
        send(4, sz.at[slot, 0], hz.at[slot, 0], up[2])
        send(5, sz.at[slot, 1], hz.at[slot, 1], down[2])
        return copies

    outer = (hx_o, hy_o, hz_o, sy_o, sz_o)
    inner = (hx_i, hy_i, hz_i, sy_i, sz_i)
    nz = right.shape[1]

    def rank_points():
        low = iota((BLK, BLK), 0) < iota((BLK, BLK), 1)
        tri = jnp.concatenate([jnp.where(low, 1.0, 0.0), jnp.ones((BLK, BLK), F32)], axis=1).astype(BF16)
        carry[...] = jnp.zeros_like(carry)
        step = next(s for s in (16, 4, 1) if blocks % s == 0)
        ids = iota((groups, BLK), 0)
        one = jnp.ones((1, BLK), F32)

        def rank_step(j, _):
            seen = carry[...]
            for b in range(step):
                at = pl.ds(pl.multiple_of((j * step + b) * BLK, BLK), BLK)
                name = dest[:, at]
                part = nn(hot_bf16(ids.astype(BF16), name, one), tri)
                rank[:, at] = jnp.sum(jnp.where(ids == name, part[:, :BLK] + seen, 0.0), axis=0, keepdims=True)
                seen = seen + part[:, BLK:]
            carry[...] = seen
            return 0

        lax.fori_loop(0, blocks // step, rank_step, 0)

    many = next(s for s in (16, 4, 1) if blocks % s == 0)

    def interpolate_all(handed, first, end):
        def go(j, _):
            for b in range(many):
                at = pl.ds(pl.multiple_of((j * many + b) * BLK, BLK), BLK)
                handed[:, at] = interpolate(field[...], nodes[:, at], lambda k: weights[k : k + 1, at], cy, nz)
            return 0

        lax.fori_loop(first, end, go, 0)

    def route():
        ids = iota((groups, BLK), 0).astype(BF16)
        slots = iota((cap, BLK), 0).astype(BF16)
        one = jnp.ones((1, BLK), F32)
        routed[...] = jnp.zeros_like(routed)

        def go(j, _):
            part = jnp.zeros(routed.shape, F32)
            for b in range(many):
                at = pl.ds(pl.multiple_of((j * many + b) * BLK, BLK), BLK)
                c = cell[:, at]
                values = (*halves(handed_r[:, at]), *halves(handed_q[:, at]), (c // 256).astype(F32), (c % 256).astype(F32))
                left = jnp.concatenate([hot_bf16(ids, dest[:, at], v) for v in values], axis=0)
                part = part + nt(left, hot_bf16(slots, rank[:, at], one))
            routed[...] += part
            return 0

        lax.fori_loop(0, blocks // many, go, 0)
        rows = [routed[pl.ds(i * groups, groups)] for i in range(6)]
        tx[...] = jnp.concatenate([rows[0] + rows[1], rows[2] + rows[3], rows[4] * 256.0 + rows[5]], axis=1).reshape(
            groups, 1, 3 * cap
        )

    middle = groups // 2

    def exchange(src, dst):
        def go(i, _):
            half = (i + 1) // 2
            t, to = peer(middle + jnp.where(lax.rem(i, 2) == 1, half, -half))
            pltpu.make_async_remote_copy(
                src.at[t], dst.at[me], a2a_send, a2a_recv, device_id=to, device_id_type=MESH
            ).start()
            return 0

        lax.fori_loop(0, groups - 1, go, 0)
        dst[pl.ds(me, 1)] = src[pl.ds(me, 1)]

    def exchanged(dst):
        all_but_one = pl.ds(0, groups - 1)
        pltpu.make_async_copy(dst.at[all_but_one], dst.at[all_but_one], a2a_recv).wait()

    def exchange_sent(src):
        all_but_one = pl.ds(0, groups - 1)
        pltpu.make_async_copy(src.at[all_but_one], src.at[all_but_one], a2a_send).wait()

    batch = next(s for s in (16, 8, 4, 2, 1) if groups % s == 0)
    ni, nzi = source.shape

    def scatter(c0, c1):
        rows_id = iota((ni, cap), 0).astype(BF16)
        cols_id = iota((nzi, cap), 0).astype(BF16)
        one = jnp.ones((1, cap), F32)
        acc[...] = jnp.zeros_like(acc)

        def go(j, _):
            part = jnp.zeros(acc.shape, F32)
            for b in range(batch):
                got = rx[j * batch + b]
                c = got[:, 2 * cap :].astype(I32)
                hi, lo = halves(c0 * got[:, :cap] + c1 * got[:, cap : 2 * cap])
                left = jnp.concatenate([hot_bf16(rows_id, c // nzi, hi), hot_bf16(rows_id, c // nzi, lo)], axis=0)
                part = part + nt(left, hot_bf16(cols_id, c % nzi, one))
            acc[...] += part
            return 0

        lax.fori_loop(0, groups // batch, go, 0)

    loads[0].wait()
    pack_halo(right, sy_o, sz_o, cy, 0)
    pl.semaphore_wait(barrier, groups - 1 + len(others))
    first = send_halo(0, right, *outer, 0)
    field[...] = field_of(right[...])
    loads[2].wait()
    loads[3].wait()
    interpolate_all(handed_r, 0, blocks // many)

    loads[4].wait()
    r = right[...]
    near = (6.0 + odiag[...]) * r - near_sum(r, cy)
    for c in first:
        c.wait_recv()
    q0[...] = near - far_sum(r.shape, hx_o[0], hy_o[0], hz_o[0], at_ends)
    pack_halo(q0, sy_o, sz_o, cy, 1)
    second = send_halo(2, q0, *outer, 1)
    field[...] = field_of(q0[...])
    loads[1].wait()
    rank_points()
    half = blocks // many // 2
    interpolate_all(handed_q, 0, half)

    q = q0[...]
    near = (6.0 + odiag[...]) * q - near_sum(q, cy)
    for c in second:
        c.wait_recv()
    q1[...] = near - far_sum(q.shape, hx_o[1], hy_o[1], hz_o[1], at_ends)
    row8 = iota((8, LANE), 0)
    packed = jnp.zeros((8, LANE), F32)
    r, qq = right[...], q1[...]
    for k, (a, b) in enumerate(((r, r), (r, q), (q, q), (q, qq))):
        s = jnp.sum((a * b).reshape(-1, 8, nz), axis=0)
        t = s[:, :LANE]
        for m in range(LANE, nz, LANE):
            t = t + s[:, m : m + LANE]
        packed = jnp.where(row8 == k, jnp.sum(t, axis=0, keepdims=True), packed)
    packed = jnp.broadcast_to(jnp.sum(packed, axis=1, keepdims=True), (8, LANE))

    def all_to_one(value, buf, mine, partners, which):
        buf[pl.ds(mine, 1)] = value[None]
        for to in partners:
            pltpu.make_async_remote_copy(
                buf.at[mine], buf.at[mine], ar_send.at[which], ar_recv.at[which], device_id=to, device_id_type=MESH
            ).start()

    def all_arrived(buf, which):
        n = buf.shape[0]
        pltpu.make_async_copy(buf.at[pl.ds(0, n - 1)], buf.at[pl.ds(0, n - 1)], ar_recv.at[which]).wait()
        s, e = buf[0], jnp.zeros((8, LANE), F32)
        for i in range(1, n):
            s, d = two_sum(s, buf[i])
            e = e + d
        return s + jnp.where(row8 >= 4, pltpu.roll(e, 4, 0), 0.0)

    def all_sent(buf, which):
        n = buf.shape[0]
        pltpu.make_async_copy(buf.at[pl.ds(0, n - 1)], buf.at[pl.ds(0, n - 1)], ar_send.at[which]).wait()

    all_to_one(packed, ar1, mx, [(lax.rem(mx + k, ngx), my, mz) for k in along], 0)

    interpolate_all(handed_q, half, blocks // many)
    loads[5].wait()
    route()
    exchange(tx, rx)
    loads[6].wait()
    pack_halo(prev, sy_i, sz_i, iy, 0)
    prev_halo = send_halo(1, prev, *inner, 0)
    all_to_one(all_arrived(ar1, 0), ar2, my * ngz + mz, [beside(a, b) for a, b in side], 1)
    loads[7].wait()
    loads[8].wait()
    inv[...] = 1.0 / (6.0 + idiag[...])
    v = prev[...]
    p1[...] = source[...] + near_sum(v, iy)
    for c in prev_halo:
        c.wait_recv()
    p1[...] += far_sum(v.shape, hx_i[0], hy_i[0], hz_i[0], at_ends)

    mu_rows = all_arrived(ar2, 1)
    mu = [(mu_rows[k : k + 1], mu_rows[4 + k : 5 + k]) for k in range(4)]
    a0 = mu[0][0] / mu[1][0]
    rr1 = dd_add(mu[0], dd_times(dd_add(dd_times(mu[2], a0), (-2.0 * mu[1][0], -2.0 * mu[1][1])), a0))
    rr1 = rr1[0] + rr1[1]
    beta = rr1 / mu[0][0]
    g = 1.0 + beta
    curve = dd_times(dd_add(dd_times(mu[1], g), dd_times(mu[2], -2.0 * a0)), g)
    curve = dd_add(curve, dd_times(dd_times(mu[3], a0), a0))
    a1 = rr1 / (curve[0] + curve[1])
    c0, c1 = (a0 + a1 * g)[:, :1], (-a0 * a1)[:, :1]
    a0, a1, beta = a0[:, :1], a1[:, :1], beta[:, :1]

    exchanged(rx)
    scatter(c0, c1)
    added = acc[pl.ds(0, ni)] + acc[pl.ds(ni, ni)]
    p1[...] = (p1[...] + added) * inv[...]
    pack_halo(p1, sy_i, sz_i, iy, 1)
    last = send_halo(3, p1, *inner, 1)
    r, q = right[...], q0[...]
    r1 = r - a0 * q
    x_out[...] = a0 * r + a1 * (r1 + beta * r)
    res_out[...] = r1 - a1 * ((q - a0 * q1[...]) + beta * q)
    stores = [
        pltpu.make_async_copy(x_out, x_hbm, store_sem.at[0]),
        pltpu.make_async_copy(res_out, res_hbm, store_sem.at[1]),
    ]
    for c in stores:
        c.start()
    near = source[...] + added + near_sum(p1[...], iy)
    for c in last:
        c.wait_recv()
    p_out[...] = (near + far_sum(near.shape, hx_i[1], hy_i[1], hz_i[1], at_ends)) * inv[...]
    c = pltpu.make_async_copy(p_out, p_hbm, store_sem.at[2])
    c.start()
    stores.append(c)
    for c in first + prev_halo + second + last:
        c.wait_send()
    exchange_sent(tx)
    all_sent(ar1, 0)
    all_sent(ar2, 1)
    for c in stores:
        c.wait()


def solution(mesh):
    ngx, ngy, ngz = (mesh.shape[a] for a in ("gx", "gy", "gz"))
    groups = ngx * ngy

    def per_device(right, odiag, nodes, weights, dest, cell, prev, source, idiag):
        cx, cy, nz = right.shape
        ix, iy, nzi = source.shape
        points = nodes.shape[0]
        cap = 2 * points // groups
        no, ni = cx * cy, ix * iy
        v = pltpu.VMEM
        dma = pltpu.SemaphoreType.DMA
        scratch = [
            v((no, nz), F32), v((no, nz), F32), v((1, points), I32), v((8, points), F32), v((1, points), I32),
            v((1, points), I32), v((ni, nzi), F32), v((ni, nzi), F32), v((ni, nzi), F32), dma((9,)),
            v((no, nz), F32), v((no, nz), F32), v((ni, nzi), F32), v((no, nz), F32), v((no, nz), F32), v((ni, nzi), F32), dma((3,)),
            v((2, 2, cy, nz), F32), v((2, 2, cx, nz), F32), v((2, 2, 8, LANE), F32), v((2, 2, cx, nz), F32), v((2, 2, 8, LANE), F32),
            v((2, 2, iy, nzi), F32), v((2, 2, ix, nzi), F32), v((2, 2, 8, LANE), F32), v((2, 2, ix, nzi), F32), v((2, 2, 8, LANE), F32),
            dma((4, 6)), dma((4, 6)),
            v((ngx, 8, LANE), F32), v((ngy * ngz, 8, LANE), F32), dma((2,)), dma((2,)),
            v((groups, 1, 3 * cap), F32), v((groups, 1, 3 * cap), F32), dma(()), dma(()),
            v((1, points), F32), v((groups, BLK), F32), v((4 * no, nz), BF16), v((1, points), F32), v((1, points), F32),
            v((6 * groups, cap), F32), v((2 * ni, nzi), F32), v((ni, nzi), F32),
        ]
        x, res, p = pl.pallas_call(
            functools.partial(kernel, (ngx, ngy, ngz, cy, iy)),
            out_shape=(
                jax.ShapeDtypeStruct((no, nz), F32),
                jax.ShapeDtypeStruct((no, nz), F32),
                jax.ShapeDtypeStruct((ni, nzi), F32),
            ),
            in_specs=[pl.BlockSpec(memory_space=pl.ANY)] * 9,
            out_specs=[pl.BlockSpec(memory_space=pl.ANY)] * 3,
            scratch_shapes=scratch,
            compiler_params=pltpu.CompilerParams(
                collective_id=0, has_side_effects=True, vmem_limit_bytes=56 * 2**20
            ),
        )(
            right.reshape(no, nz), odiag.reshape(no, nz), nodes.reshape(1, points), weights,
            dest.reshape(1, points), cell.reshape(1, points), prev.reshape(ni, nzi),
            source.reshape(ni, nzi), idiag.reshape(ni, nzi),
        )
        return x.reshape(cx, cy, nz), res.reshape(cx, cy, nz), p.reshape(ix, iy, nzi)

    block = P("gx", "gy", "gz")
    every = ("gx", "gy", "gz")
    return jax.shard_map(
        per_device,
        mesh=mesh,
        in_specs=(block, block, P(every), P(None, every), P(every, None), P(every), block, block, block),
        out_specs=(block, block, block),
        check_vma=False,
    )
```

time: 58.6 us -> 44.8 us (0.76)
  Pallas kernels: 54.9 us -> 41 us
    pallas_call x1, Pallas kernels: 54.9 us -> 41 us  [per_device(): pl.pallas_call(functools.partial(kernel, (ngx, ngy, ngz, cy, iy)), out_sh...]
where the time goes in v2:
time: 44.8 us; the launch traced here: 44.7 us
  Pallas kernels  41 us (92%)
  local copies, waits for them, and re-layouts  2.98 us (7%)
  between operations  0.66 us (1%)
    pallas_call x1, Pallas kernels, per_device(): pl.pallas_call(functools.partial(kernel, (ngx, ngy, ngz, cy, iy)), out_sh...  41 us
    unnamed x7, local copies, waits for them, and re-layouts  2.98 us

profile of v2, /device:TPU:1, one launch (start us, length us, event | category | flops | bytes accessed | tf_op | source)
XLA Modules:
  0.0 44.7 jit_solution(290120113886316246)
XLA Ops:
  0.6 41.0 %shard_map.112 = (f32[128,256]{1,0:T(8,128)}, f32[128,256]{1,0:T(8,128)}, f32[256,256]{1,0:T(8,128)}) custom-call(f32[128,256]{1,0:T(8,128)} %bitcast.17, f32[128,256]{1,0:T(8,128)} %bitcast.18, s32[1,8192]{1,0:T(1,128)} %bitcast.19, f32[8,8192]{1,0:T(8,128)} %weights_hbm.1, s32[1,8192]{1,0:T(1,128)} %bitcast.20, s32[1,8192]{1,0:T(1,128)} %bitcast.21, ...), custom_call_target="tpu_custom_call" | custom-call | tf_op jit(solution)/shard_map/pallas_call | solution.py:489
  41.7 0.0 copy-start.1
  41.7 0.0 copy-start
  41.7 1.6 %copy.15 = f32[8,16,256]{2,1,0:T(8,128)} copy(f32[8,16,256]{2,1,0:T(8,128)} %bitcast.16) | data formatting | bytes 262144
  43.3 0.0 copy-done.1
  43.3 0.7 %copy.16 = f32[8,16,256]{2,1,0:T(8,128)} copy(f32[8,16,256]{2,1,0:T(8,128)S(1)} %bitcast.15) | data formatting | bytes 262144
  44.0 0.0 copy-done
  44.0 0.7 %copy.17 = f32[8,32,256]{2,1,0:T(8,128)} copy(f32[8,32,256]{2,1,0:T(8,128)S(1)} %bitcast.11) | data formatting | bytes 524288
Async XLA Ops:
  41.7 1.6 %copy-start.1 = (f32[128,256]{1,0:T(8,128)S(1)}, f32[128,256]{1,0:T(8,128)}, u32[]{:S(2)}) copy-start(f32[128,256]{1,0:T(8,128)} %get-tuple-element.7) | copy-start | bytes 393220
  41.7 2.3 %copy-start = (f32[256,256]{1,0:T(8,128)S(1)}, f32[256,256]{1,0:T(8,128)}, u32[]{:S(2)}) copy-start(f32[256,256]{1,0:T(8,128)} %get-tuple-element.8) | copy-start | bytes 786436

commit v3 on v2

--- a/solution.py
+++ b/solution.py
@@ -158,7 +158,7 @@
     q0, q1, p1, x_out, res_out, p_out, store_sem,
     hx_o, hy_o, hz_o, sy_o, sz_o, hx_i, hy_i, hz_i, sy_i, sz_i, halo_send, halo_recv,
     ar1, ar2, ar_send, ar_recv,
-    tx, rx, a2a_send, a2a_recv,
+    tx, rx, a2a_send, a2a_recv, ready,
     rank, carry, field, handed_r, handed_q, routed, acc, inv,
 ):
     ngx, ngy, ngz, cy, iy = sizes
@@ -176,10 +176,6 @@
         t = lax.rem(me + k, groups)
         return t, (t // ngy, lax.rem(t, ngy), mz)
 
-    def greet_peer(k, _):
-        pl.semaphore_signal(barrier, inc=1, device_id=peer(k)[1], device_id_type=MESH)
-        return 0
-
     loads = []
     for i, (a, b) in enumerate(
         ((right_hbm, right), (dest_hbm, dest), (nodes_hbm, nodes), (weights_hbm, weights), (odiag_hbm, odiag),
@@ -188,7 +184,6 @@
         c = pltpu.make_async_copy(a, b, load_sem.at[i])
         c.start()
         loads.append(c)
-    lax.fori_loop(1, groups, greet_peer, 0)
     side = [(a, b) for a in range(ngy) for b in range(ngz) if (a, b) != (0, 0)]
     side.sort(key=lambda t: -(min(t[0], ngy - t[0]) + min(t[1], ngz - t[1])))
     along = sorted(range(1, ngx), key=lambda k: -min(k, ngx - k))
@@ -196,9 +191,10 @@
     def beside(a, b):
         return (mx, lax.rem(my + a, ngy), lax.rem(mz + b, ngz))
 
-    others = [(a, b) for a, b in side if b]
-    for a, b in others:
-        pl.semaphore_signal(barrier, inc=1, device_id=beside(a, b), device_id_type=MESH)
+    line = [(lax.rem(mx + k, ngx), my, mz) for k in along]
+    layer = [beside(a, b) for a, b in side]
+    for to in line + layer:
+        pl.semaphore_signal(barrier, inc=1, device_id=to, device_id_type=MESH)
 
     up = ((lax.rem(mx + 1, ngx), my, mz), (mx, lax.rem(my + 1, ngy), mz), (mx, my, lax.rem(mz + 1, ngz)))
     down = (
@@ -341,12 +337,16 @@
 
     loads[0].wait()
     pack_halo(right, sy_o, sz_o, cy, 0)
-    pl.semaphore_wait(barrier, groups - 1 + len(others))
+    pl.semaphore_wait(barrier, len(line) + len(layer))
     first = send_halo(0, right, *outer, 0)
+    for to in line:
+        pl.semaphore_signal(ready, inc=1, device_id=to, device_id_type=MESH)
     field[...] = field_of(right[...])
     loads[2].wait()
     loads[3].wait()
     interpolate_all(handed_r, 0, blocks // many)
+    loads[1].wait()
+    rank_points()
 
     loads[4].wait()
     r = right[...]
@@ -357,10 +357,7 @@
     pack_halo(q0, sy_o, sz_o, cy, 1)
     second = send_halo(2, q0, *outer, 1)
     field[...] = field_of(q0[...])
-    loads[1].wait()
-    rank_points()
-    half = blocks // many // 2
-    interpolate_all(handed_q, 0, half)
+    interpolate_all(handed_q, 0, blocks // many)
 
     q = q0[...]
     near = (6.0 + odiag[...]) * q - near_sum(q, cy)
@@ -398,16 +395,16 @@
         n = buf.shape[0]
         pltpu.make_async_copy(buf.at[pl.ds(0, n - 1)], buf.at[pl.ds(0, n - 1)], ar_send.at[which]).wait()
 
-    all_to_one(packed, ar1, mx, [(lax.rem(mx + k, ngx), my, mz) for k in along], 0)
-
-    interpolate_all(handed_q, half, blocks // many)
+    all_to_one(packed, ar1, mx, line, 0)
+
     loads[5].wait()
     route()
+    pl.semaphore_wait(ready, len(line))
     exchange(tx, rx)
     loads[6].wait()
     pack_halo(prev, sy_i, sz_i, iy, 0)
     prev_halo = send_halo(1, prev, *inner, 0)
-    all_to_one(all_arrived(ar1, 0), ar2, my * ngz + mz, [beside(a, b) for a, b in side], 1)
+    all_to_one(all_arrived(ar1, 0), ar2, my * ngz + mz, layer, 1)
     loads[7].wait()
     loads[8].wait()
     inv[...] = 1.0 / (6.0 + idiag[...])
@@ -482,7 +479,7 @@
             v((2, 2, iy, nzi), F32), v((2, 2, ix, nzi), F32), v((2, 2, 8, LANE), F32), v((2, 2, ix, nzi), F32), v((2, 2, 8, LANE), F32),
             dma((4, 6)), dma((4, 6)),
             v((ngx, 8, LANE), F32), v((ngy * ngz, 8, LANE), F32), dma((2,)), dma((2,)),
-            v((groups, 1, 3 * cap), F32), v((groups, 1, 3 * cap), F32), dma(()), dma(()),
+            v((groups, 1, 3 * cap), F32), v((groups, 1, 3 * cap), F32), dma(()), dma(()), pltpu.SemaphoreType.REGULAR,
             v((1, points), F32), v((groups, BLK), F32), v((4 * no, nz), BF16), v((1, points), F32), v((1, points), F32),
             v((6 * groups, cap), F32), v((2 * ni, nzi), F32), v((ni, nzi), F32),
         ]

time: 44.8 us -> 43.7 us (0.975)
  Pallas kernels: 41 us -> 39.9 us
    pallas_call x1, Pallas kernels: 41 us -> 39.9 us  [per_device(): pl.pallas_call(functools.partial(kernel, (ngx, ngy, ngz, cy, iy)), out_sh...]
where the time goes in v3:
time: 43.7 us; the launch traced here: 43.6 us
  Pallas kernels  39.9 us (91%)
  local copies, waits for them, and re-layouts  2.98 us (7%)
  between operations  0.66 us (2%)
    pallas_call x1, Pallas kernels, per_device(): pl.pallas_call(functools.partial(kernel, (ngx, ngy, ngz, cy, iy)), out_sh...  39.9 us
    unnamed x7, local copies, waits for them, and re-layouts  2.98 us

profile of v3, /device:TPU:1, one launch (start us, length us, event | category | flops | bytes accessed | tf_op | source)
XLA Modules:
  0.0 43.6 jit_solution(4353787529256449398)
XLA Ops:
  0.6 39.9 %shard_map.112 = (f32[128,256]{1,0:T(8,128)}, f32[128,256]{1,0:T(8,128)}, f32[256,256]{1,0:T(8,128)}) custom-call(f32[128,256]{1,0:T(8,128)} %bitcast.17, f32[128,256]{1,0:T(8,128)} %bitcast.18, s32[1,8192]{1,0:T(1,128)} %bitcast.19, f32[8,8192]{1,0:T(8,128)} %weights_hbm.1, s32[1,8192]{1,0:T(1,128)} %bitcast.20, s32[1,8192]{1,0:T(1,128)} %bitcast.21, ...), custom_call_target="tpu_custom_call" | custom-call | tf_op jit(solution)/shard_map/pallas_call | solution.py:486
  40.6 0.0 copy-start.1
  40.6 0.0 copy-start
  40.6 1.6 %copy.15 = f32[8,16,256]{2,1,0:T(8,128)} copy(f32[8,16,256]{2,1,0:T(8,128)} %bitcast.16) | data formatting | bytes 262144
  42.2 0.0 copy-done.1
  42.2 0.7 %copy.16 = f32[8,16,256]{2,1,0:T(8,128)} copy(f32[8,16,256]{2,1,0:T(8,128)S(1)} %bitcast.15) | data formatting | bytes 262144
  42.9 0.0 copy-done
  42.9 0.7 %copy.17 = f32[8,32,256]{2,1,0:T(8,128)} copy(f32[8,32,256]{2,1,0:T(8,128)S(1)} %bitcast.11) | data formatting | bytes 524288
Async XLA Ops:
  40.6 1.6 %copy-start.1 = (f32[128,256]{1,0:T(8,128)S(1)}, f32[128,256]{1,0:T(8,128)}, u32[]{:S(2)}) copy-start(f32[128,256]{1,0:T(8,128)} %get-tuple-element.7) | copy-start | bytes 393220
  40.6 2.3 %copy-start = (f32[256,256]{1,0:T(8,128)S(1)}, f32[256,256]{1,0:T(8,128)}, u32[]{:S(2)}) copy-start(f32[256,256]{1,0:T(8,128)} %get-tuple-element.8) | copy-start | bytes 786436

commit v4 on v3

--- a/solution.py
+++ b/solution.py
@@ -292,28 +292,30 @@
         )
 
     middle = groups // 2
+    batch = next(s for s in (16, 8, 4, 2, 1) if groups % s == 0)
+
+    def offset(i):
+        half = (i + 1) // 2
+        return middle + jnp.where(lax.rem(i, 2) == 1, half, -half)
 
     def exchange(src, dst):
         def go(i, _):
-            half = (i + 1) // 2
-            t, to = peer(middle + jnp.where(lax.rem(i, 2) == 1, half, -half))
+            t, to = peer(offset(i))
             pltpu.make_async_remote_copy(
-                src.at[t], dst.at[me], a2a_send, a2a_recv, device_id=to, device_id_type=MESH
+                src.at[t], dst.at[me], a2a_send, a2a_recv.at[i // batch], device_id=to, device_id_type=MESH
             ).start()
             return 0
 
         lax.fori_loop(0, groups - 1, go, 0)
-        dst[pl.ds(me, 1)] = src[pl.ds(me, 1)]
-
-    def exchanged(dst):
-        all_but_one = pl.ds(0, groups - 1)
-        pltpu.make_async_copy(dst.at[all_but_one], dst.at[all_but_one], a2a_recv).wait()
+        pltpu.make_async_copy(src.at[me], dst.at[me], a2a_recv.at[groups // batch - 1]).start()
+
+    def exchanged(dst, j):
+        pltpu.make_async_copy(dst.at[pl.ds(0, batch)], dst.at[pl.ds(0, batch)], a2a_recv.at[j]).wait()
 
     def exchange_sent(src):
         all_but_one = pl.ds(0, groups - 1)
         pltpu.make_async_copy(src.at[all_but_one], src.at[all_but_one], a2a_send).wait()
 
-    batch = next(s for s in (16, 8, 4, 2, 1) if groups % s == 0)
     ni, nzi = source.shape
 
     def scatter(c0, c1):
@@ -323,9 +325,10 @@
         acc[...] = jnp.zeros_like(acc)
 
         def go(j, _):
+            exchanged(rx, j)
             part = jnp.zeros(acc.shape, F32)
             for b in range(batch):
-                got = rx[j * batch + b]
+                got = rx[lax.rem(me + 2 * groups - offset(j * batch + b), groups)]
                 c = got[:, 2 * cap :].astype(I32)
                 hi, lo = halves(c0 * got[:, :cap] + c1 * got[:, cap : 2 * cap])
                 left = jnp.concatenate([hot_bf16(rows_id, c // nzi, hi), hot_bf16(rows_id, c // nzi, lo)], axis=0)
@@ -337,16 +340,16 @@
 
     loads[0].wait()
     pack_halo(right, sy_o, sz_o, cy, 0)
+    field[...] = field_of(right[...])
+    loads[1].wait()
+    rank_points()
     pl.semaphore_wait(barrier, len(line) + len(layer))
     first = send_halo(0, right, *outer, 0)
     for to in line:
         pl.semaphore_signal(ready, inc=1, device_id=to, device_id_type=MESH)
-    field[...] = field_of(right[...])
     loads[2].wait()
     loads[3].wait()
     interpolate_all(handed_r, 0, blocks // many)
-    loads[1].wait()
-    rank_points()
 
     loads[4].wait()
     r = right[...]
@@ -427,7 +430,6 @@
     c0, c1 = (a0 + a1 * g)[:, :1], (-a0 * a1)[:, :1]
     a0, a1, beta = a0[:, :1], a1[:, :1], beta[:, :1]
 
-    exchanged(rx)
     scatter(c0, c1)
     added = acc[pl.ds(0, ni)] + acc[pl.ds(ni, ni)]
     p1[...] = (p1[...] + added) * inv[...]
@@ -459,6 +461,19 @@
         c.wait()
 
 
+def hand_out(x, res, p, x_hbm, res_hbm, p_hbm, x_v, res_v, p_v, sem):
+    held = ((p, p_v, p_hbm), (x, x_v, x_hbm), (res, res_v, res_hbm))
+    into = [pltpu.make_async_copy(a, b, sem.at[0, i]) for i, (a, b, _) in enumerate(held)]
+    out = [pltpu.make_async_copy(b, c, sem.at[1, i]) for i, (_, b, c) in enumerate(held)]
+    for c in into:
+        c.start()
+    for c, d in zip(into, out):
+        c.wait()
+        d.start()
+    for d in out:
+        d.wait()
+
+
 def solution(mesh):
     ngx, ngy, ngz = (mesh.shape[a] for a in ("gx", "gy", "gz"))
     groups = ngx * ngy
@@ -479,7 +494,7 @@
             v((2, 2, iy, nzi), F32), v((2, 2, ix, nzi), F32), v((2, 2, 8, LANE), F32), v((2, 2, ix, nzi), F32), v((2, 2, 8, LANE), F32),
             dma((4, 6)), dma((4, 6)),
             v((ngx, 8, LANE), F32), v((ngy * ngz, 8, LANE), F32), dma((2,)), dma((2,)),
-            v((groups, 1, 3 * cap), F32), v((groups, 1, 3 * cap), F32), dma(()), dma(()), pltpu.SemaphoreType.REGULAR,
+            v((groups, 1, 3 * cap), F32), v((groups, 1, 3 * cap), F32), dma(()), dma((4,)), pltpu.SemaphoreType.REGULAR,
             v((1, points), F32), v((groups, BLK), F32), v((4 * no, nz), BF16), v((1, points), F32), v((1, points), F32),
             v((6 * groups, cap), F32), v((2 * ni, nzi), F32), v((ni, nzi), F32),
         ]
@@ -501,6 +516,14 @@
             dest.reshape(1, points), cell.reshape(1, points), prev.reshape(ni, nzi),
             source.reshape(ni, nzi), idiag.reshape(ni, nzi),
         )
+        x, res, p = pl.pallas_call(
+            hand_out,
+            out_shape=tuple(jax.ShapeDtypeStruct(a.shape, F32) for a in (x, res, p)),
+            in_specs=[pl.BlockSpec(memory_space=pl.ANY)] * 3,
+            out_specs=[pl.BlockSpec(memory_space=pl.ANY)] * 3,
+            scratch_shapes=[v((no, nz), F32), v((no, nz), F32), v((ni, nzi), F32), dma((2, 3))],
+            compiler_params=pltpu.CompilerParams(vmem_limit_bytes=60 * 2**20),
+        )(x, res, p)
         return x.reshape(cx, cy, nz), res.reshape(cx, cy, nz), p.reshape(ix, iy, nzi)
 
     block = P("gx", "gy", "gz")

time: 43.7 us -> 40.1 us (0.918)
  local copies, waits for them, and re-layouts: 2.98 us -> 0 us
  Pallas kernels: 39.9 us -> 39.4 us
    unnamed x7 -> x0, local copies, waits for them, and re-layouts: 2.98 us -> none
    pallas_call x1, Pallas kernels: 39.9 us -> 37.6 us  [per_device(): pl.pallas_call(functools.partial(kernel, (ngx, ngy, ngz, cy, iy)), out_sh...]
    pallas_call x0 -> x1, Pallas kernels: none -> 1.79 us  [per_device(): pl.pallas_call(hand_out, out_shape=tuple((jax.ShapeDtypeStruct(a.shape, F...]
where the time goes in v4:
time: 40.1 us; the launch traced here: 40 us
  Pallas kernels  39.4 us (98%)
  between operations  0.64 us (2%)
    pallas_call x1, Pallas kernels, per_device(): pl.pallas_call(functools.partial(kernel, (ngx, ngy, ngz, cy, iy)), out_sh...  37.6 us
    pallas_call x1, Pallas kernels, per_device(): pl.pallas_call(hand_out, out_shape=tuple((jax.ShapeDtypeStruct(a.shape, F...  1.79 us

profile of v4, /device:TPU:1, one launch (start us, length us, event | category | flops | bytes accessed | tf_op | source)
XLA Modules:
  0.0 40.0 jit_solution(7968264816115583043)
XLA Ops:
  0.6 37.6 %shard_map.112 = (f32[128,256]{1,0:T(8,128)}, f32[128,256]{1,0:T(8,128)}, f32[256,256]{1,0:T(8,128)}) custom-call(f32[128,256]{1,0:T(8,128)} %bitcast.14, f32[128,256]{1,0:T(8,128)} %bitcast.15, s32[1,8192]{1,0:T(1,128)} %bitcast.16, f32[8,8192]{1,0:T(8,128)} %weights_hbm.1, s32[1,8192]{1,0:T(1,128)} %bitcast.17, s32[1,8192]{1,0:T(1,128)} %bitcast.18, ...), custom_call_target="tpu_custom_call" | custom-call | tf_op jit(solution)/shard_map/pallas_call | solution.py:501
  38.2 1.8 %shard_map.113 = (f32[128,256]{1,0:T(8,128)}, f32[128,256]{1,0:T(8,128)}, f32[256,256]{1,0:T(8,128)}) custom-call(f32[128,256]{1,0:T(8,128)} %get-tuple-element.9.x, f32[128,256]{1,0:T(8,128)} %get-tuple-element.10.res, f32[256,256]{1,0:T(8,128)} %get-tuple-element.11.p), custom_call_target="tpu_custom_call" | custom-call | tf_op jit(solution)/shard_map/pallas_call | solution.py:519

commit v5 on v4

--- a/solution.py
+++ b/solution.py
@@ -153,9 +153,9 @@
 def kernel(
     sizes,
     right_hbm, odiag_hbm, nodes_hbm, weights_hbm, dest_hbm, cell_hbm, prev_hbm, source_hbm, idiag_hbm,
-    x_hbm, res_hbm, p_hbm,
+    x_out, res_out, p_out,
     right, odiag, nodes, weights, dest, cell, prev, source, idiag, load_sem,
-    q0, q1, p1, x_out, res_out, p_out, store_sem,
+    q0, q1, p1,
     hx_o, hy_o, hz_o, sy_o, sz_o, hx_i, hy_i, hz_i, sy_i, sz_i, halo_send, halo_recv,
     ar1, ar2, ar_send, ar_recv,
     tx, rx, a2a_send, a2a_recv, ready,
@@ -439,39 +439,24 @@
     r1 = r - a0 * q
     x_out[...] = a0 * r + a1 * (r1 + beta * r)
     res_out[...] = r1 - a1 * ((q - a0 * q1[...]) + beta * q)
-    stores = [
-        pltpu.make_async_copy(x_out, x_hbm, store_sem.at[0]),
-        pltpu.make_async_copy(res_out, res_hbm, store_sem.at[1]),
-    ]
-    for c in stores:
-        c.start()
     near = source[...] + added + near_sum(p1[...], iy)
     for c in last:
         c.wait_recv()
     p_out[...] = (near + far_sum(near.shape, hx_i[1], hy_i[1], hz_i[1], at_ends)) * inv[...]
-    c = pltpu.make_async_copy(p_out, p_hbm, store_sem.at[2])
-    c.start()
-    stores.append(c)
     for c in first + prev_halo + second + last:
         c.wait_send()
     exchange_sent(tx)
     all_sent(ar1, 0)
     all_sent(ar2, 1)
-    for c in stores:
+
+
+def hand_out(x, res, p, x_hbm, res_hbm, p_hbm, sem):
+    pairs = ((p, p_hbm), (x, x_hbm), (res, res_hbm))
+    copies = [pltpu.make_async_copy(a, b, sem.at[i]) for i, (a, b) in enumerate(pairs)]
+    for c in copies:
+        c.start()
+    for c in copies:
         c.wait()
-
-
-def hand_out(x, res, p, x_hbm, res_hbm, p_hbm, x_v, res_v, p_v, sem):
-    held = ((p, p_v, p_hbm), (x, x_v, x_hbm), (res, res_v, res_hbm))
-    into = [pltpu.make_async_copy(a, b, sem.at[0, i]) for i, (a, b, _) in enumerate(held)]
-    out = [pltpu.make_async_copy(b, c, sem.at[1, i]) for i, (_, b, c) in enumerate(held)]
-    for c in into:
-        c.start()
-    for c, d in zip(into, out):
-        c.wait()
-        d.start()
-    for d in out:
-        d.wait()
 
 
 def solution(mesh):
@@ -489,7 +474,7 @@
         scratch = [
             v((no, nz), F32), v((no, nz), F32), v((1, points), I32), v((8, points), F32), v((1, points), I32),
             v((1, points), I32), v((ni, nzi), F32), v((ni, nzi), F32), v((ni, nzi), F32), dma((9,)),
-            v((no, nz), F32), v((no, nz), F32), v((ni, nzi), F32), v((no, nz), F32), v((no, nz), F32), v((ni, nzi), F32), dma((3,)),
+            v((no, nz), F32), v((no, nz), F32), v((ni, nzi), F32),
             v((2, 2, cy, nz), F32), v((2, 2, cx, nz), F32), v((2, 2, 8, LANE), F32), v((2, 2, cx, nz), F32), v((2, 2, 8, LANE), F32),
             v((2, 2, iy, nzi), F32), v((2, 2, ix, nzi), F32), v((2, 2, 8, LANE), F32), v((2, 2, ix, nzi), F32), v((2, 2, 8, LANE), F32),
             dma((4, 6)), dma((4, 6)),
@@ -500,13 +485,9 @@
         ]
         x, res, p = pl.pallas_call(
             functools.partial(kernel, (ngx, ngy, ngz, cy, iy)),
-            out_shape=(
-                jax.ShapeDtypeStruct((no, nz), F32),
-                jax.ShapeDtypeStruct((no, nz), F32),
-                jax.ShapeDtypeStruct((ni, nzi), F32),
-            ),
+            out_shape=(v((no, nz), F32), v((no, nz), F32), v((ni, nzi), F32)),
             in_specs=[pl.BlockSpec(memory_space=pl.ANY)] * 9,
-            out_specs=[pl.BlockSpec(memory_space=pl.ANY)] * 3,
+            out_specs=[pl.BlockSpec(memory_space=pltpu.VMEM)] * 3,
             scratch_shapes=scratch,
             compiler_params=pltpu.CompilerParams(
                 collective_id=0, has_side_effects=True, vmem_limit_bytes=56 * 2**20
@@ -519,10 +500,10 @@
         x, res, p = pl.pallas_call(
             hand_out,
             out_shape=tuple(jax.ShapeDtypeStruct(a.shape, F32) for a in (x, res, p)),
-            in_specs=[pl.BlockSpec(memory_space=pl.ANY)] * 3,
+            in_specs=[pl.BlockSpec(memory_space=pltpu.VMEM)] * 3,
             out_specs=[pl.BlockSpec(memory_space=pl.ANY)] * 3,
-            scratch_shapes=[v((no, nz), F32), v((no, nz), F32), v((ni, nzi), F32), dma((2, 3))],
-            compiler_params=pltpu.CompilerParams(vmem_limit_bytes=60 * 2**20),
+            scratch_shapes=[dma((3,))],
+            compiler_params=pltpu.CompilerParams(vmem_limit_bytes=32 * 2**20),
         )(x, res, p)
         return x.reshape(cx, cy, nz), res.reshape(cx, cy, nz), p.reshape(ix, iy, nzi)
 

time: 40.1 us -> 38.5 us (0.960)
  Pallas kernels: 39.4 us -> 37.7 us
    pallas_call x1, Pallas kernels: 1.79 us -> 0.81 us  [per_device(): pl.pallas_call(hand_out, out_shape=tuple((jax.ShapeDtypeStruct(a.shape, F...]
    pallas_call x1, Pallas kernels: 37.6 us -> 36.9 us  [per_device(): pl.pallas_call(functools.partial(kernel, (ngx, ngy, ngz, cy, iy)), out_sh...]
where the time goes in v5:
time: 38.5 us; the launch traced here: 38.4 us
  Pallas kernels  37.7 us (98%)
  between operations  0.64 us (2%)
    pallas_call x1, Pallas kernels, per_device(): pl.pallas_call(functools.partial(kernel, (ngx, ngy, ngz, cy, iy)), out_sh...  36.9 us
    pallas_call x1, Pallas kernels, per_device(): pl.pallas_call(hand_out, out_shape=tuple((jax.ShapeDtypeStruct(a.shape, F...  0.81 us

profile of v5, /device:TPU:1, one launch (start us, length us, event | category | flops | bytes accessed | tf_op | source)
XLA Modules:
  0.0 38.4 jit_solution(6685293856938657201)
XLA Ops:
  0.6 36.9 %shard_map.112 = (f32[128,256]{1,0:T(8,128)S(1)}, f32[128,256]{1,0:T(8,128)S(1)}, f32[256,256]{1,0:T(8,128)S(1)}) custom-call(f32[128,256]{1,0:T(8,128)} %bitcast.14, f32[128,256]{1,0:T(8,128)} %bitcast.15, s32[1,8192]{1,0:T(1,128)} %bitcast.16, f32[8,8192]{1,0:T(8,128)} %weights_hbm.1, s32[1,8192]{1,0:T(1,128)} %bitcast.17, s32[1,8192]{1,0:T(1,128)} %bitcast.18, ...), custom_call_target="tpu_custom_call" | custom-call | tf_op jit(solution)/shard_map/pallas_call | solution.py:486
  37.6 0.8 %shard_map.113 = (f32[128,256]{1,0:T(8,128)}, f32[128,256]{1,0:T(8,128)}, f32[256,256]{1,0:T(8,128)}) custom-call(f32[128,256]{1,0:T(8,128)S(1)} %get-tuple-element.9.x, f32[128,256]{1,0:T(8,128)S(1)} %get-tuple-element.10.res, f32[256,256]{1,0:T(8,128)S(1)} %get-tuple-element.11.p), custom_call_target="tpu_custom_call" | custom-call | tf_op jit(solution)/shard_map/pallas_call | solution.py:500

commit v6 on v5

--- a/solution.py
+++ b/solution.py
@@ -203,16 +203,18 @@
         (mx, my, lax.rem(mz + ngz - 1, ngz)),
     )
 
-    def pack_halo(src, sy, sz, ny, slot):
-        rows, nz = src.shape
+    def pack_y(src, sy, ny, slot):
         v = src[...]
-        solid = v.reshape(rows // ny, ny, nz)
+        solid = v.reshape(v.shape[0] // ny, ny, v.shape[1])
         sy[slot, 0] = solid[:, ny - 1, :]
         sy[slot, 1] = solid[:, 0, :]
-        sz[slot, 0] = column(v, nz - 1)
+
+    def pack_z(src, sz, slot):
+        v = src[...]
+        sz[slot, 0] = column(v, v.shape[1] - 1)
         sz[slot, 1] = column(v, 0)
 
-    def send_halo(which, src, hx, hy, hz, sy, sz, slot):
+    def send_halo(which, src, hx, hy, hz, sy, sz, slot, packed=False):
         rows = src.shape[0]
         ny = hx.shape[2]
         copies = []
@@ -226,8 +228,12 @@
 
         send(0, src.at[pl.ds(rows - ny, ny)], hx.at[slot, 0], up[0])
         send(1, src.at[pl.ds(0, ny)], hx.at[slot, 1], down[0])
+        if not packed:
+            pack_y(src, sy, ny, slot)
         send(2, sy.at[slot, 0], hy.at[slot, 0], up[1])
         send(3, sy.at[slot, 1], hy.at[slot, 1], down[1])
+        if not packed:
+            pack_z(src, sz, slot)
         send(4, sz.at[slot, 0], hz.at[slot, 0], up[2])
         send(5, sz.at[slot, 1], hz.at[slot, 1], down[2])
         return copies
@@ -339,12 +345,13 @@
         lax.fori_loop(0, groups // batch, go, 0)
 
     loads[0].wait()
-    pack_halo(right, sy_o, sz_o, cy, 0)
+    pack_y(right, sy_o, cy, 0)
+    pack_z(right, sz_o, 0)
     field[...] = field_of(right[...])
     loads[1].wait()
     rank_points()
     pl.semaphore_wait(barrier, len(line) + len(layer))
-    first = send_halo(0, right, *outer, 0)
+    first = send_halo(0, right, *outer, 0, packed=True)
     for to in line:
         pl.semaphore_signal(ready, inc=1, device_id=to, device_id_type=MESH)
     loads[2].wait()
@@ -357,26 +364,29 @@
     for c in first:
         c.wait_recv()
     q0[...] = near - far_sum(r.shape, hx_o[0], hy_o[0], hz_o[0], at_ends)
-    pack_halo(q0, sy_o, sz_o, cy, 1)
     second = send_halo(2, q0, *outer, 1)
     field[...] = field_of(q0[...])
     interpolate_all(handed_q, 0, blocks // many)
 
     q = q0[...]
     near = (6.0 + odiag[...]) * q - near_sum(q, cy)
+    row8 = iota((8, LANE), 0)
+
+    def folded(a, b):
+        t = jnp.sum((a * b).reshape(-1, 8, nz), axis=0)
+        t = sum((t[:, m : m + LANE] for m in range(LANE, nz, LANE)), t[:, :LANE])
+        return jnp.sum(t, axis=0, keepdims=True)
+
+    r = right[...]
+    packed = jnp.zeros((8, LANE), F32)
+    for k, (a, b) in enumerate(((r, r), (r, q), (q, q))):
+        packed = jnp.where(row8 == k, folded(a, b), packed)
     for c in second:
         c.wait_recv()
-    q1[...] = near - far_sum(q.shape, hx_o[1], hy_o[1], hz_o[1], at_ends)
-    row8 = iota((8, LANE), 0)
-    packed = jnp.zeros((8, LANE), F32)
-    r, qq = right[...], q1[...]
-    for k, (a, b) in enumerate(((r, r), (r, q), (q, q), (q, qq))):
-        s = jnp.sum((a * b).reshape(-1, 8, nz), axis=0)
-        t = s[:, :LANE]
-        for m in range(LANE, nz, LANE):
-            t = t + s[:, m : m + LANE]
-        packed = jnp.where(row8 == k, jnp.sum(t, axis=0, keepdims=True), packed)
+    qq = near - far_sum(q.shape, hx_o[1], hy_o[1], hz_o[1], at_ends)
+    packed = jnp.where(row8 == 3, folded(q, qq), packed)
     packed = jnp.broadcast_to(jnp.sum(packed, axis=1, keepdims=True), (8, LANE))
+    q1[...] = qq
 
     def all_to_one(value, buf, mine, partners, which):
         buf[pl.ds(mine, 1)] = value[None]
@@ -388,10 +398,12 @@
     def all_arrived(buf, which):
         n = buf.shape[0]
         pltpu.make_async_copy(buf.at[pl.ds(0, n - 1)], buf.at[pl.ds(0, n - 1)], ar_recv.at[which]).wait()
-        s, e = buf[0], jnp.zeros((8, LANE), F32)
-        for i in range(1, n):
-            s, d = two_sum(s, buf[i])
-            e = e + d
+        terms = [(buf[i], jnp.zeros((8, LANE), F32)) for i in range(n)]
+        while len(terms) > 1:
+            odd = terms[len(terms) // 2 * 2 :]
+            pairs = [(*two_sum(x[0], y[0]), x[1] + y[1]) for x, y in zip(terms[::2], terms[1::2])]
+            terms = [(t, d + e) for t, d, e in pairs] + odd
+        s, e = terms[0]
         return s + jnp.where(row8 >= 4, pltpu.roll(e, 4, 0), 0.0)
 
     def all_sent(buf, which):
@@ -405,7 +417,6 @@
     pl.semaphore_wait(ready, len(line))
     exchange(tx, rx)
     loads[6].wait()
-    pack_halo(prev, sy_i, sz_i, iy, 0)
     prev_halo = send_halo(1, prev, *inner, 0)
     all_to_one(all_arrived(ar1, 0), ar2, my * ngz + mz, layer, 1)
     loads[7].wait()
@@ -433,7 +444,6 @@
     scatter(c0, c1)
     added = acc[pl.ds(0, ni)] + acc[pl.ds(ni, ni)]
     p1[...] = (p1[...] + added) * inv[...]
-    pack_halo(p1, sy_i, sz_i, iy, 1)
     last = send_halo(3, p1, *inner, 1)
     r, q = right[...], q0[...]
     r1 = r - a0 * q

time: 38.5 us -> 38.1 us (0.990)
    pallas_call x1, Pallas kernels: 36.9 us -> 36.5 us  [per_device(): pl.pallas_call(functools.partial(kernel, (ngx, ngy, ngz, cy, iy)), out_sh...]
where the time goes in v6:
time: 38.1 us; the launch traced here: 38 us
  Pallas kernels  37.4 us (98%)
  between operations  0.64 us (2%)
    pallas_call x1, Pallas kernels, per_device(): pl.pallas_call(functools.partial(kernel, (ngx, ngy, ngz, cy, iy)), out_sh...  36.5 us
    pallas_call x1, Pallas kernels, per_device(): pl.pallas_call(hand_out, out_shape=tuple((jax.ShapeDtypeStruct(a.shape, F...  0.81 us

profile of v6, /device:TPU:1, one launch (start us, length us, event | category | flops | bytes accessed | tf_op | source)
XLA Modules:
  0.0 38.0 jit_solution(8829435911586387872)
XLA Ops:
  0.6 36.5 %shard_map.112 = (f32[128,256]{1,0:T(8,128)S(1)}, f32[128,256]{1,0:T(8,128)S(1)}, f32[256,256]{1,0:T(8,128)S(1)}) custom-call(f32[128,256]{1,0:T(8,128)} %bitcast.14, f32[128,256]{1,0:T(8,128)} %bitcast.15, s32[1,8192]{1,0:T(1,128)} %bitcast.16, f32[8,8192]{1,0:T(8,128)} %weights_hbm.1, s32[1,8192]{1,0:T(1,128)} %bitcast.17, s32[1,8192]{1,0:T(1,128)} %bitcast.18, ...), custom_call_target="tpu_custom_call" | custom-call | tf_op jit(solution)/shard_map/pallas_call | solution.py:496
  37.2 0.8 %shard_map.113 = (f32[128,256]{1,0:T(8,128)}, f32[128,256]{1,0:T(8,128)}, f32[256,256]{1,0:T(8,128)}) custom-call(f32[128,256]{1,0:T(8,128)S(1)} %get-tuple-element.9.x, f32[128,256]{1,0:T(8,128)S(1)} %get-tuple-element.10.res, f32[256,256]{1,0:T(8,128)S(1)} %get-tuple-element.11.p), custom_call_target="tpu_custom_call" | custom-call | tf_op jit(solution)/shard_map/pallas_call | solution.py:510
